TPU v7x, 256 devices: a whole 4x4x8 slice. The times are simulated.
256 devices in a mesh: shift: 4 (over y_lo, core), band: 4 (over z_lo), lane: 16 (over z_hi, y_hi, x).
Axes of the slice: x: 4, y: 4 (y_hi: 2, y_lo: 2; y = y_hi * 2 + y_lo), z: 8 (z_hi: 2, z_lo: 4; z = z_hi * 4 + z_lo), core: 2. Of those that a mesh axis runs over, the one named last changes fastest.
Arguments:
- source_terms: float32 [1024, 1024, 128], P(('shift', 'band'), 'lane'), parts along dimension 0, may hold values from -6 to 6
- initial_values: float32 [1024, 1024, 128], P(('shift', 'band'), 'lane'), parts along dimension 0, may hold values from -6 to 6
- absorption: float32 [1024, 1024, 128], P(('shift', 'band'), 'lane'), parts along dimension 0, may hold values from 0.1 to 0.9
Outputs:
- corrected: float32 [1024, 1024, 128], P(('shift', 'band'), 'lane'), parts along dimension 0
There are 4 independent parts, one for each index of `shift`. A program takes and returns all parts, laid end to end along the dimension named above; each array names one. Nothing has to cross between parts.
All inputs are finite; a program needn't handle non-finite values.
Results may differ from a plain program's by a relative error of at most 0.0003.
Values sent between devices are 32-bit elements.
A program may use at most 64 MiB of HBM per device.

v0:
```python
import jax
import jax.numpy as jnp
from jax import lax
from jax.sharding import PartitionSpec as P

RATIO = 2
BEFORE = 3
AFTER = 3
INNER = 13


def with_halo(block, sides, width, periodic):
    for axis, dim in sides:
        count = lax.axis_size(axis)
        forward = [(i, i + 1) for i in range(count - 1)]
        if periodic:
            forward.append((count - 1, 0))
        backward = [(target, source) for source, target in forward]
        low = lax.ppermute(
            lax.slice_in_dim(block, block.shape[dim] - width, None, axis=dim), axis, forward
        )
        high = lax.ppermute(lax.slice_in_dim(block, 0, width, axis=dim), axis, backward)
        block = jnp.concatenate([low, block, high], axis=dim)
    return block


def neighbour_sum(padded):
    inner_y, inner_x = (padded.shape[0] - 2, padded.shape[1] - 2)
    middle_rows = lax.slice_in_dim(padded, 1, 1 + inner_y, axis=0)
    middle_columns = lax.slice_in_dim(padded, 1, 1 + inner_x, axis=1)
    return (
        lax.slice_in_dim(middle_columns, 0, inner_y, axis=0)
        + lax.slice_in_dim(middle_columns, 2, 2 + inner_y, axis=0)
        + lax.slice_in_dim(middle_rows, 0, inner_x, axis=1)
        + lax.slice_in_dim(middle_rows, 2, 2 + inner_x, axis=1)
    )


def sweep_once(padded, values, load, mass_here):
    return values + 0.8 * (load + neighbour_sum(padded) - (4.0 + mass_here) * values) / (
        4.0 + mass_here
    )


def block_means(values):
    cut = values.reshape(
        values.shape[0] // RATIO, RATIO, values.shape[1] // RATIO, RATIO, values.shape[2]
    )
    return jnp.mean(cut, axis=(1, 3))


def spread_blocks(values):
    return jnp.repeat(jnp.repeat(values, RATIO, axis=0), RATIO, axis=1)


def without_rim(values):
    return lax.slice_in_dim(
        lax.slice_in_dim(values, 1, values.shape[0] - 1, axis=0), 1, values.shape[1] - 1, axis=1
    )


def per_device(source_terms, initial_values, absorption):
    values = initial_values
    for sweep in range(BEFORE):
        values = sweep_once(
            with_halo(values, (("band", 0), ("lane", 1)), 1, False),
            values,
            source_terms,
            absorption,
        )
    defect = (
        source_terms
        + neighbour_sum(with_halo(values, (("band", 0), ("lane", 1)), 1, False))
        - (4.0 + absorption) * values
    )
    coarse_load, coarse_mass = (block_means(defect) * RATIO, block_means(absorption) * RATIO)
    coarse_values = 0.8 * coarse_load / (4.0 + coarse_mass)
    depth = 2
    load_mass = with_halo(
        jnp.concatenate([coarse_load, coarse_mass], axis=2), (("band", 0), ("lane", 1)), 2, False
    )
    wide_load, wide_mass = jnp.split(load_mass, 2, axis=2)
    place_y = (
        lax.axis_index("band") * coarse_load.shape[0]
        - depth
        + jnp.arange(coarse_load.shape[0] + 2 * depth)
    )
    place_x = (
        lax.axis_index("lane") * coarse_load.shape[1]
        - depth
        + jnp.arange(coarse_load.shape[1] + 2 * depth)
    )
    inside_y = (place_y >= 0) & (place_y < coarse_load.shape[0] * lax.axis_size("band"))
    inside_x = (place_x >= 0) & (place_x < coarse_load.shape[1] * lax.axis_size("lane"))
    inside = (inside_y[:, None] & inside_x[None, :])[:, :, None]
    for group in range((INNER - 1) // 2):
        wide_values = with_halo(coarse_values, (("band", 0), ("lane", 1)), 2, False)
        once = sweep_once(
            wide_values, without_rim(wide_values), without_rim(wide_load), without_rim(wide_mass)
        )
        once = jnp.where(without_rim(inside), once, 0.0)
        middle = without_rim(once)
        coarse_values = sweep_once(once, middle, coarse_load, coarse_mass)
    values = values + spread_blocks(coarse_values)
    for sweep in range(AFTER):
        values = sweep_once(
            with_halo(values, (("band", 0), ("lane", 1)), 1, False),
            values,
            source_terms,
            absorption,
        )
    corrected = values
    return corrected


def solution(mesh):
    placed = (
        P(("shift", "band"), "lane", None),
        P(("shift", "band"), "lane", None),
        P(("shift", "band"), "lane", None),
    )
    return jax.shard_map(
        per_device,
        mesh=mesh,
        in_specs=placed,
        out_specs=P(("shift", "band"), "lane", None),
        check_vma=False,
    )
```

profile of v0, /device:TPU:54, one launch (start us, length us, event | category | flops | bytes accessed | tf_op | source)
XLA Modules:
  0.0 401.7 jit_solution(926837576587092164)
XLA Ops:
  10.5 7.0 %collective-permute-start.2 = (f32[66,1,128]{2,1,0:T(1,128)S(1)}, f32[66,1,128]{2,1,0:T(1,128)S(1)}, u32[]{:S(2)}, u32[]{:S(2)}) collective-permute-start(f32[66,1,128]{2,1,0:T(1,128)S(1)} %get-tuple-element.20), channel_id=1, source_target_pairs={{0,1},{1,2},{2,3},{3,4},{4,5},{5,6},{6,7},{7,8},{8,9},{9,10},{10,1... | collective-permute-start | bytes 101384 | tf_op jit(solution)/shard_map/ppermute | solution.py:19
  19.5 12.8 %collective-permute-done.3 = f32[66,1,128]{2,1,0:T(1,128)S(1)} collective-permute-done((f32[66,1,128]{2,1,0:T(1,128)S(1)}, f32[66,1,128]{2,1,0:T(1,128)S(1)}, u32[]{:S(2)}, u32[]{:S(2)}) %collective-permute-start.3) | collective-permute-done | bytes 33824 | tf_op jit(solution)/shard_map/ppermute | solution.py:22
  32.4 5.8 %fusion.50 = f32[64,64,128]{2,1,0:T(8,128)S(1)} fusion(f32[64,64,128]{2,1,0:T(8,128)} %param.4, f32[64,64,128]{2,1,0:T(8,128)S(1)} %copy-done.1, f32[66,1,128]{2,1,0:T(1,128)S(1)} %collective-permute-done.3, f32[66,64,128]{2,1,0:T(8,128)S(1)} %constant_dynamic-update-slice_fusion, f32[66,1,128]{2,1,0:T(1,128)S(1)} %collective-permute-done.2, ...), kind=kLoop, calls=%fused_computation.99 | loop fusion | flops 7340032 | bytes 10684416 | tf_op jit(solution)/shard_map/add | solution.py:40
  48.3 3.9 collective-permute-start.7
  52.2 10.3 %collective-permute-done.7 = f32[66,1,128]{2,1,0:T(1,128)S(1)} collective-permute-done((f32[66,1,128]{2,1,0:T(1,128)S(1)}, f32[66,1,128]{2,1,0:T(1,128)S(1)}, u32[]{:S(2)}, u32[]{:S(2)}) %collective-permute-start.7) | collective-permute-done | bytes 33824 | tf_op jit(solution)/shard_map/ppermute | solution.py:22
  62.5 8.6 %fusion.42 = f32[64,64,128]{2,1,0:T(8,128)S(1)} fusion(f32[64,64,128]{2,1,0:T(8,128)} %copy-done.7, f32[64,64,128]{2,1,0:T(8,128)} %param.3, f32[66,1,128]{2,1,0:T(1,128)S(1)} %collective-permute-done.7, f32[1,64,128]{2,1,0:T(8,128)S(1)} %collective-permute-done.5, f32[1,64,128]{2,1,0:T(8,128)S(1)} %collective-permute-done.4, ...), kind=kLoop, calls=%fused_computation.83 | loop fusion | flops 9437184 | bytes 8521728 | tf_op jit(solution)/shard_map/add | solution.py:40
  83.3 3.9 collective-permute-start.11
  87.3 10.2 %collective-permute-done.11 = f32[66,1,128]{2,1,0:T(1,128)S(1)} collective-permute-done((f32[66,1,128]{2,1,0:T(1,128)S(1)}, f32[66,1,128]{2,1,0:T(1,128)S(1)}, u32[]{:S(2)}, u32[]{:S(2)}) %collective-permute-start.11) | collective-permute-done | bytes 33824 | tf_op jit(solution)/shard_map/ppermute | solution.py:22
  97.5 8.0 %fusion.34 = f32[64,64,128]{2,1,0:T(8,128)S(1)} fusion(f32[64,64,128]{2,1,0:T(8,128)} %copy-done.6, f32[64,64,128]{2,1,0:T(8,128)S(1)} %copy-done.2, f32[66,1,128]{2,1,0:T(1,128)S(1)} %collective-permute-done.11, f32[1,64,128]{2,1,0:T(8,128)S(1)} %collective-permute-done.9, f32[1,64,128]{2,1,0:T(8,128)S(1)} %collective-permute-done.8, ...), kind=kLoop, calls=%fused_computation.67 | loop fusion | flops 9437184 | bytes 8521728 | tf_op jit(solution)/shard_map/add | solution.py:40
  107.5 3.9 collective-permute-start.13
  115.3 3.9 collective-permute-start.15
  120.9 8.6 %collective-permute-done.15 = f32[66,1,128]{2,1,0:T(1,128)S(1)} collective-permute-done((f32[66,1,128]{2,1,0:T(1,128)S(1)}, f32[66,1,128]{2,1,0:T(1,128)S(1)}, u32[]{:S(2)}, u32[]{:S(2)}) %collective-permute-start.15) | collective-permute-done | bytes 33824 | tf_op jit(solution)/shard_map/ppermute | solution.py:22
  129.5 9.3 %fusion.26 = f32[64,64,128]{2,1,0:T(8,128)} fusion(f32[64,64,128]{2,1,0:T(8,128)} %param.3, f32[66,1,128]{2,1,0:T(1,128)S(1)} %collective-permute-done.15, f32[1,64,128]{2,1,0:T(8,128)S(1)} %collective-permute-done.13, f32[64,64,128]{2,1,0:T(8,128)} %copy-done.4, f32[1,64,128]{2,1,0:T(8,128)S(1)} %collective-permute-done.12, ...), kind=kLoop, calls=%fused_computation.51 | loop fusion | flops 7864320 | bytes 8521728 | tf_op jit(solution)/shard_map/sub | solution.py:72
  156.2 3.9 collective-permute-start.19
  160.2 10.3 %collective-permute-start.22 = (f32[36,2,256]{2,1,0:T(2,128)S(1)}, f32[36,2,256]{2,1,0:T(2,128)S(1)}, u32[]{:S(2)}, u32[]{:S(2)}) collective-permute-start(f32[36,2,256]{2,1,0:T(2,128)S(1)} %get-tuple-element.36), channel_id=1, source_target_pairs={{0,1},{1,2},{2,3},{3,4},{4,5},{5,6},{6,7},{7,8},{8,9},{9,10},{10,1... | collective-permute-start | bytes 221192 | tf_op jit(solution)/shard_map/ppermute | solution.py:19
  172.6 12.6 %collective-permute-done.23 = f32[36,2,256]{2,1,0:T(2,128)S(1)} collective-permute-done((f32[36,2,256]{2,1,0:T(2,128)S(1)}, f32[36,2,256]{2,1,0:T(2,128)S(1)}, u32[]{:S(2)}, u32[]{:S(2)}) %collective-permute-start.23) | collective-permute-done | bytes 73760 | tf_op jit(solution)/shard_map/ppermute | solution.py:22
  198.4 3.9 collective-permute-start.27
  202.3 10.3 %collective-permute-done.27 = f32[36,2,128]{2,1,0:T(2,128)S(1)} collective-permute-done((f32[36,2,128]{2,1,0:T(2,128)S(1)}, f32[36,2,128]{2,1,0:T(2,128)S(1)}, u32[]{:S(2)}, u32[]{:S(2)}) %collective-permute-start.27) | collective-permute-done | bytes 36896 | tf_op jit(solution)/shard_map/ppermute | solution.py:22
  227.8 10.4 %collective-permute-done.31 = f32[36,2,128]{2,1,0:T(2,128)S(1)} collective-permute-done((f32[36,2,128]{2,1,0:T(2,128)S(1)}, f32[36,2,128]{2,1,0:T(2,128)S(1)}, u32[]{:S(2)}, u32[]{:S(2)}) %collective-permute-start.31) | collective-permute-done | bytes 36896 | tf_op jit(solution)/shard_map/ppermute | solution.py:22
  249.5 3.9 collective-permute-start.35
  253.4 10.3 %collective-permute-done.35 = f32[36,2,128]{2,1,0:T(2,128)S(1)} collective-permute-done((f32[36,2,128]{2,1,0:T(2,128)S(1)}, f32[36,2,128]{2,1,0:T(2,128)S(1)}, u32[]{:S(2)}, u32[]{:S(2)}) %collective-permute-start.35) | collective-permute-done | bytes 36896 | tf_op jit(solution)/shard_map/ppermute | solution.py:22
  275.0 3.9 collective-permute-start.39
  278.9 10.3 %collective-permute-done.39 = f32[36,2,128]{2,1,0:T(2,128)S(1)} collective-permute-done((f32[36,2,128]{2,1,0:T(2,128)S(1)}, f32[36,2,128]{2,1,0:T(2,128)S(1)}, u32[]{:S(2)}, u32[]{:S(2)}) %collective-permute-start.39) | collective-permute-done | bytes 36896 | tf_op jit(solution)/shard_map/ppermute | solution.py:22
  300.5 3.9 collective-permute-start.43
  304.4 10.3 %collective-permute-done.43 = f32[36,2,128]{2,1,0:T(2,128)S(1)} collective-permute-done((f32[36,2,128]{2,1,0:T(2,128)S(1)}, f32[36,2,128]{2,1,0:T(2,128)S(1)}, u32[]{:S(2)}, u32[]{:S(2)}) %collective-permute-start.43) | collective-permute-done | bytes 36896 | tf_op jit(solution)/shard_map/ppermute | solution.py:22
  328.3 3.9 collective-permute-start.47
  332.2 10.4 %collective-permute-done.47 = f32[66,1,128]{2,1,0:T(1,128)S(1)} collective-permute-done((f32[66,1,128]{2,1,0:T(1,128)S(1)}, f32[66,1,128]{2,1,0:T(1,128)S(1)}, u32[]{:S(2)}, u32[]{:S(2)}) %collective-permute-start.47) | collective-permute-done | bytes 33824 | tf_op jit(solution)/shard_map/ppermute | solution.py:22
  355.7 4.1 %collective-permute-start.51 = (f32[66,1,128]{2,1,0:T(1,128)S(1)}, f32[66,1,128]{2,1,0:T(1,128)S(1)}, u32[]{:S(2)}, u32[]{:S(2)}) collective-permute-start(f32[66,1,128]{2,1,0:T(1,128)S(1)} %get-tuple-element.11), channel_id=1, source_target_pairs={{1,0},{2,1},{3,2},{4,3},{5,4},{6,5},{7,6},{8,7},{9,8},{10,9},{11,1... | collective-permute-start | bytes 101384 | tf_op jit(solution)/shard_map/ppermute | solution.py:22
  359.9 10.1 %collective-permute-done.51 = f32[66,1,128]{2,1,0:T(1,128)S(1)} collective-permute-done((f32[66,1,128]{2,1,0:T(1,128)S(1)}, f32[66,1,128]{2,1,0:T(1,128)S(1)}, u32[]{:S(2)}, u32[]{:S(2)}) %collective-permute-start.51) | collective-permute-done | bytes 33824 | tf_op jit(solution)/shard_map/ppermute | solution.py:22
  383.1 3.9 collective-permute-start.55
  387.1 10.3 %collective-permute-done.55 = f32[66,1,128]{2,1,0:T(1,128)S(1)} collective-permute-done((f32[66,1,128]{2,1,0:T(1,128)S(1)}, f32[66,1,128]{2,1,0:T(1,128)S(1)}, u32[]{:S(2)}, u32[]{:S(2)}) %collective-permute-start.55) | collective-permute-done | bytes 33824 | tf_op jit(solution)/shard_map/ppermute | solution.py:22
  397.4 4.3 %fusion.5 = f32[64,64,128]{2,1,0:T(8,128)} fusion(f32[64,64,128]{2,1,0:T(8,128)S(1)} %fusion.13, f32[64,64,128]{2,1,0:T(8,128)S(1)} %copy-done.3, f32[66,1,128]{2,1,0:T(1,128)S(1)} %collective-permute-done.55, f32[1,64,128]{2,1,0:T(8,128)S(1)} %collective-permute-done.53, f32[1,64,128]{2,1,0:T(8,128)S(1)} %collective-permute-done.52, ...), kind=kLoop, calls=%fused_computation.6 | loop fusion | flops 9437184 | bytes 8521728 | tf_op jit(solution)/shard_map/add | solution.py:40
  (163 shorter events, 162.9 us)
Async XLA Ops:
  10.5 9.1 %collective-permute-start.2 = (f32[66,1,128]{2,1,0:T(1,128)S(1)}, f32[66,1,128]{2,1,0:T(1,128)S(1)}, u32[]{:S(2)}, u32[]{:S(2)}) collective-permute-start(f32[66,1,128]{2,1,0:T(1,128)S(1)} %get-tuple-element.20), channel_id=1, source_target_pairs={{0,1},{1,2},{2,3},{3,4},{4,5},{5,6},{6,7},{7,8},{8,9},{9,10},{10,1... | collective-permute-start | bytes 101384 | tf_op jit(solution)/shard_map/ppermute | solution.py:19
  17.5 14.9 %collective-permute-start.3 = (f32[66,1,128]{2,1,0:T(1,128)S(1)}, f32[66,1,128]{2,1,0:T(1,128)S(1)}, u32[]{:S(2)}, u32[]{:S(2)}) collective-permute-start(f32[66,1,128]{2,1,0:T(1,128)S(1)} %get-tuple-element.21), channel_id=1, source_target_pairs={{1,0},{2,1},{3,2},{4,3},{5,4},{6,5},{7,6},{8,7},{9,8},{10,9},{11,1... | collective-permute-start | bytes 101384 | tf_op jit(solution)/shard_map/ppermute | solution.py:22
  46.3 5.9 %collective-permute-start.6 = (f32[66,1,128]{2,1,0:T(1,128)S(1)}, f32[66,1,128]{2,1,0:T(1,128)S(1)}, u32[]{:S(2)}, u32[]{:S(2)}) collective-permute-start(f32[66,1,128]{2,1,0:T(1,128)S(1)} %get-tuple-element.18), channel_id=1, source_target_pairs={{0,1},{1,2},{2,3},{3,4},{4,5},{5,6},{6,7},{7,8},{8,9},{9,10},{10,1... | collective-permute-start | bytes 101384 | tf_op jit(solution)/shard_map/ppermute | solution.py:19
  48.3 14.2 %collective-permute-start.7 = (f32[66,1,128]{2,1,0:T(1,128)S(1)}, f32[66,1,128]{2,1,0:T(1,128)S(1)}, u32[]{:S(2)}, u32[]{:S(2)}) collective-permute-start(f32[66,1,128]{2,1,0:T(1,128)S(1)} %get-tuple-element.19), channel_id=1, source_target_pairs={{1,0},{2,1},{3,2},{4,3},{5,4},{6,5},{7,6},{8,7},{9,8},{10,9},{11,1... | collective-permute-start | bytes 101384 | tf_op jit(solution)/shard_map/ppermute | solution.py:22
  72.5 5.9 %collective-permute-start.8 = (f32[1,64,128]{2,1,0:T(8,128)S(1)}, f32[1,64,128]{2,1,0:T(8,128)S(1)}, u32[]{:S(2)}, u32[]{:S(2)}) collective-permute-start(f32[1,64,128]{2,1,0:T(8,128)S(1)} %get-tuple-element.30), channel_id=1, source_target_pairs={{0,16},{16,32},{32,48},{1,17},{17,33},{33,49},{2,18},{18,34},{34,5... | collective-permute-start | bytes 98312 | tf_op jit(solution)/shard_map/ppermute | solution.py:19
  81.3 6.0 %collective-permute-start.10 = (f32[66,1,128]{2,1,0:T(1,128)S(1)}, f32[66,1,128]{2,1,0:T(1,128)S(1)}, u32[]{:S(2)}, u32[]{:S(2)}) collective-permute-start(f32[66,1,128]{2,1,0:T(1,128)S(1)} %get-tuple-element.16), channel_id=1, source_target_pairs={{0,1},{1,2},{2,3},{3,4},{4,5},{5,6},{6,7},{7,8},{8,9},{9,10},{10,1... | collective-permute-start | bytes 101384 | tf_op jit(solution)/shard_map/ppermute | solution.py:19
  83.3 14.2 %collective-permute-start.11 = (f32[66,1,128]{2,1,0:T(1,128)S(1)}, f32[66,1,128]{2,1,0:T(1,128)S(1)}, u32[]{:S(2)}, u32[]{:S(2)}) collective-permute-start(f32[66,1,128]{2,1,0:T(1,128)S(1)} %get-tuple-element.17), channel_id=1, source_target_pairs={{1,0},{2,1},{3,2},{4,3},{5,4},{6,5},{7,6},{8,7},{9,8},{10,9},{11,1... | collective-permute-start | bytes 101384 | tf_op jit(solution)/shard_map/ppermute | solution.py:22
  105.6 5.9 %collective-permute-start.12 = (f32[1,64,128]{2,1,0:T(8,128)S(1)}, f32[1,64,128]{2,1,0:T(8,128)S(1)}, u32[]{:S(2)}, u32[]{:S(2)}) collective-permute-start(f32[1,64,128]{2,1,0:T(8,128)S(1)} %get-tuple-element.28), channel_id=1, source_target_pairs={{0,16},{16,32},{32,48},{1,17},{17,33},{33,49},{2,18},{18,34},{34,5... | collective-permute-start | bytes 98312 | tf_op jit(solution)/shard_map/ppermute | solution.py:19
  113.3 7.6 %collective-permute-start.14 = (f32[66,1,128]{2,1,0:T(1,128)S(1)}, f32[66,1,128]{2,1,0:T(1,128)S(1)}, u32[]{:S(2)}, u32[]{:S(2)}) collective-permute-start(f32[66,1,128]{2,1,0:T(1,128)S(1)} %get-tuple-element.14), channel_id=1, source_target_pairs={{0,1},{1,2},{2,3},{3,4},{4,5},{5,6},{6,7},{7,8},{8,9},{9,10},{10,1... | collective-permute-start | bytes 101384 | tf_op jit(solution)/shard_map/ppermute | solution.py:19
  115.3 14.2 %collective-permute-start.15 = (f32[66,1,128]{2,1,0:T(1,128)S(1)}, f32[66,1,128]{2,1,0:T(1,128)S(1)}, u32[]{:S(2)}, u32[]{:S(2)}) collective-permute-start(f32[66,1,128]{2,1,0:T(1,128)S(1)} %get-tuple-element.15), channel_id=1, source_target_pairs={{1,0},{2,1},{3,2},{4,3},{5,4},{6,5},{7,6},{8,7},{9,8},{10,9},{11,1... | collective-permute-start | bytes 101384 | tf_op jit(solution)/shard_map/ppermute | solution.py:22
  142.3 11.7 %collective-permute-start.16 = (f32[2,32,128]{2,1,0:T(8,128)S(1)}, f32[2,32,128]{2,1,0:T(8,128)S(1)}, u32[]{:S(2)}, u32[]{:S(2)}) collective-permute-start(f32[2,32,128]{2,1,0:T(8,128)S(1)} %get-tuple-element.65), channel_id=1, source_target_pairs={{0,16},{16,32},{32,48},{1,17},{17,33},{33,49},{2,18},{18,34},{34,5... | collective-permute-start | bytes 98312 | tf_op jit(solution)/shard_map/ppermute | solution.py:19
  144.3 9.8 %collective-permute-start.17 = (f32[2,32,128]{2,1,0:T(8,128)S(1)}, f32[2,32,128]{2,1,0:T(8,128)S(1)}, u32[]{:S(2)}, u32[]{:S(2)}) collective-permute-start(f32[2,32,128]{2,1,0:T(8,128)S(1)} %get-tuple-element.66), channel_id=1, source_target_pairs={{16,0},{32,16},{48,32},{17,1},{33,17},{49,33},{18,2},{34,18},{50,3... | collective-permute-start | bytes 98312 | tf_op jit(solution)/shard_map/ppermute | solution.py:22
  148.2 12.0 %collective-permute-start.20 = (f32[2,32,256]{2,1,0:T(8,128)S(1)}, f32[2,32,256]{2,1,0:T(8,128)S(1)}, u32[]{:S(2)}, u32[]{:S(2)}) collective-permute-start(f32[2,32,256]{2,1,0:T(8,128)S(1)} %get-tuple-element.38), channel_id=1, source_target_pairs={{0,16},{16,32},{32,48},{1,17},{17,33},{33,49},{2,18},{18,34},{34,5... | collective-permute-start | bytes 196616 | tf_op jit(solution)/shard_map/ppermute | solution.py:19
  150.1 10.0 %collective-permute-start.21 = (f32[2,32,256]{2,1,0:T(8,128)S(1)}, f32[2,32,256]{2,1,0:T(8,128)S(1)}, u32[]{:S(2)}, u32[]{:S(2)}) collective-permute-start(f32[2,32,256]{2,1,0:T(8,128)S(1)} %get-tuple-element.39), channel_id=1, source_target_pairs={{16,0},{32,16},{48,32},{17,1},{33,17},{49,33},{18,2},{34,18},{50,3... | collective-permute-start | bytes 196616 | tf_op jit(solution)/shard_map/ppermute | solution.py:22
  154.1 18.4 %collective-permute-start.18 = (f32[36,2,128]{2,1,0:T(2,128)S(1)}, f32[36,2,128]{2,1,0:T(2,128)S(1)}, u32[]{:S(2)}, u32[]{:S(2)}) collective-permute-start(f32[36,2,128]{2,1,0:T(2,128)S(1)} %get-tuple-element.50), channel_id=1, source_target_pairs={{0,1},{1,2},{2,3},{3,4},{4,5},{5,6},{6,7},{7,8},{8,9},{9,10},{10,1... | collective-permute-start | bytes 110600 | tf_op jit(solution)/shard_map/ppermute | solution.py:19
  156.2 16.3 %collective-permute-start.19 = (f32[36,2,128]{2,1,0:T(2,128)S(1)}, f32[36,2,128]{2,1,0:T(2,128)S(1)}, u32[]{:S(2)}, u32[]{:S(2)}) collective-permute-start(f32[36,2,128]{2,1,0:T(2,128)S(1)} %get-tuple-element.51), channel_id=1, source_target_pairs={{1,0},{2,1},{3,2},{4,3},{5,4},{6,5},{7,6},{8,7},{9,8},{10,9},{11,1... | collective-permute-start | bytes 110600 | tf_op jit(solution)/shard_map/ppermute | solution.py:22
  160.2 12.4 %collective-permute-start.22 = (f32[36,2,256]{2,1,0:T(2,128)S(1)}, f32[36,2,256]{2,1,0:T(2,128)S(1)}, u32[]{:S(2)}, u32[]{:S(2)}) collective-permute-start(f32[36,2,256]{2,1,0:T(2,128)S(1)} %get-tuple-element.36), channel_id=1, source_target_pairs={{0,1},{1,2},{2,3},{3,4},{4,5},{5,6},{6,7},{7,8},{8,9},{9,10},{10,1... | collective-permute-start | bytes 221192 | tf_op jit(solution)/shard_map/ppermute | solution.py:19
  170.6 14.7 %collective-permute-start.23 = (f32[36,2,256]{2,1,0:T(2,128)S(1)}, f32[36,2,256]{2,1,0:T(2,128)S(1)}, u32[]{:S(2)}, u32[]{:S(2)}) collective-permute-start(f32[36,2,256]{2,1,0:T(2,128)S(1)} %get-tuple-element.37), channel_id=1, source_target_pairs={{1,0},{2,1},{3,2},{4,3},{5,4},{6,5},{7,6},{8,7},{9,8},{10,9},{11,1... | collective-permute-start | bytes 221192 | tf_op jit(solution)/shard_map/ppermute | solution.py:22
  196.5 5.9 %collective-permute-start.26 = (f32[36,2,128]{2,1,0:T(2,128)S(1)}, f32[36,2,128]{2,1,0:T(2,128)S(1)}, u32[]{:S(2)}, u32[]{:S(2)}) collective-permute-start(f32[36,2,128]{2,1,0:T(2,128)S(1)} %get-tuple-element.48), channel_id=1, source_target_pairs={{0,1},{1,2},{2,3},{3,4},{4,5},{5,6},{6,7},{7,8},{8,9},{9,10},{10,1... | collective-permute-start | bytes 110600 | tf_op jit(solution)/shard_map/ppermute | solution.py:19
  198.4 14.3 %collective-permute-start.27 = (f32[36,2,128]{2,1,0:T(2,128)S(1)}, f32[36,2,128]{2,1,0:T(2,128)S(1)}, u32[]{:S(2)}, u32[]{:S(2)}) collective-permute-start(f32[36,2,128]{2,1,0:T(2,128)S(1)} %get-tuple-element.49), channel_id=1, source_target_pairs={{1,0},{2,1},{3,2},{4,3},{5,4},{6,5},{7,6},{8,7},{9,8},{10,9},{11,1... | collective-permute-start | bytes 110600 | tf_op jit(solution)/shard_map/ppermute | solution.py:22
  222.0 5.9 %collective-permute-start.30 = (f32[36,2,128]{2,1,0:T(2,128)S(1)}, f32[36,2,128]{2,1,0:T(2,128)S(1)}, u32[]{:S(2)}, u32[]{:S(2)}) collective-permute-start(f32[36,2,128]{2,1,0:T(2,128)S(1)} %get-tuple-element.46), channel_id=1, source_target_pairs={{0,1},{1,2},{2,3},{3,4},{4,5},{5,6},{6,7},{7,8},{8,9},{9,10},{10,1... | collective-permute-start | bytes 110600 | tf_op jit(solution)/shard_map/ppermute | solution.py:19
  224.0 14.3 %collective-permute-start.31 = (f32[36,2,128]{2,1,0:T(2,128)S(1)}, f32[36,2,128]{2,1,0:T(2,128)S(1)}, u32[]{:S(2)}, u32[]{:S(2)}) collective-permute-start(f32[36,2,128]{2,1,0:T(2,128)S(1)} %get-tuple-element.47), channel_id=1, source_target_pairs={{1,0},{2,1},{3,2},{4,3},{5,4},{6,5},{7,6},{8,7},{9,8},{10,9},{11,1... | collective-permute-start | bytes 110600 | tf_op jit(solution)/shard_map/ppermute | solution.py:22
  247.6 5.9 %collective-permute-start.34 = (f32[36,2,128]{2,1,0:T(2,128)S(1)}, f32[36,2,128]{2,1,0:T(2,128)S(1)}, u32[]{:S(2)}, u32[]{:S(2)}) collective-permute-start(f32[36,2,128]{2,1,0:T(2,128)S(1)} %get-tuple-element.44), channel_id=1, source_target_pairs={{0,1},{1,2},{2,3},{3,4},{4,5},{5,6},{6,7},{7,8},{8,9},{9,10},{10,1... | collective-permute-start | bytes 110600 | tf_op jit(solution)/shard_map/ppermute | solution.py:19
  249.5 14.3 %collective-permute-start.35 = (f32[36,2,128]{2,1,0:T(2,128)S(1)}, f32[36,2,128]{2,1,0:T(2,128)S(1)}, u32[]{:S(2)}, u32[]{:S(2)}) collective-permute-start(f32[36,2,128]{2,1,0:T(2,128)S(1)} %get-tuple-element.45), channel_id=1, source_target_pairs={{1,0},{2,1},{3,2},{4,3},{5,4},{6,5},{7,6},{8,7},{9,8},{10,9},{11,1... | collective-permute-start | bytes 110600 | tf_op jit(solution)/shard_map/ppermute | solution.py:22
  273.1 5.9 %collective-permute-start.38 = (f32[36,2,128]{2,1,0:T(2,128)S(1)}, f32[36,2,128]{2,1,0:T(2,128)S(1)}, u32[]{:S(2)}, u32[]{:S(2)}) collective-permute-start(f32[36,2,128]{2,1,0:T(2,128)S(1)} %get-tuple-element.42), channel_id=1, source_target_pairs={{0,1},{1,2},{2,3},{3,4},{4,5},{5,6},{6,7},{7,8},{8,9},{9,10},{10,1... | collective-permute-start | bytes 110600 | tf_op jit(solution)/shard_map/ppermute | solution.py:19
  275.0 14.3 %collective-permute-start.39 = (f32[36,2,128]{2,1,0:T(2,128)S(1)}, f32[36,2,128]{2,1,0:T(2,128)S(1)}, u32[]{:S(2)}, u32[]{:S(2)}) collective-permute-start(f32[36,2,128]{2,1,0:T(2,128)S(1)} %get-tuple-element.43), channel_id=1, source_target_pairs={{1,0},{2,1},{3,2},{4,3},{5,4},{6,5},{7,6},{8,7},{9,8},{10,9},{11,1... | collective-permute-start | bytes 110600 | tf_op jit(solution)/shard_map/ppermute | solution.py:22
  300.5 14.3 %collective-permute-start.43 = (f32[36,2,128]{2,1,0:T(2,128)S(1)}, f32[36,2,128]{2,1,0:T(2,128)S(1)}, u32[]{:S(2)}, u32[]{:S(2)}) collective-permute-start(f32[36,2,128]{2,1,0:T(2,128)S(1)} %get-tuple-element.41), channel_id=1, source_target_pairs={{1,0},{2,1},{3,2},{4,3},{5,4},{6,5},{7,6},{8,7},{9,8},{10,9},{11,1... | collective-permute-start | bytes 110600 | tf_op jit(solution)/shard_map/ppermute | solution.py:22
  318.5 6.0 %collective-permute-start.44 = (f32[1,64,128]{2,1,0:T(8,128)S(1)}, f32[1,64,128]{2,1,0:T(8,128)S(1)}, u32[]{:S(2)}, u32[]{:S(2)}) collective-permute-start(f32[1,64,128]{2,1,0:T(8,128)S(1)} %get-tuple-element.26), channel_id=1, source_target_pairs={{0,16},{16,32},{32,48},{1,17},{17,33},{33,49},{2,18},{18,34},{34,5... | collective-permute-start | bytes 98312 | tf_op jit(solution)/shard_map/ppermute | solution.py:19
  328.3 14.3 %collective-permute-start.47 = (f32[66,1,128]{2,1,0:T(1,128)S(1)}, f32[66,1,128]{2,1,0:T(1,128)S(1)}, u32[]{:S(2)}, u32[]{:S(2)}) collective-permute-start(f32[66,1,128]{2,1,0:T(1,128)S(1)} %get-tuple-element.13), channel_id=1, source_target_pairs={{1,0},{2,1},{3,2},{4,3},{5,4},{6,5},{7,6},{8,7},{9,8},{10,9},{11,1... | collective-permute-start | bytes 101384 | tf_op jit(solution)/shard_map/ppermute | solution.py:22
  353.8 6.1 %collective-permute-start.50 = (f32[66,1,128]{2,1,0:T(1,128)S(1)}, f32[66,1,128]{2,1,0:T(1,128)S(1)}, u32[]{:S(2)}, u32[]{:S(2)}) collective-permute-start(f32[66,1,128]{2,1,0:T(1,128)S(1)} %get-tuple-element.10), channel_id=1, source_target_pairs={{0,1},{1,2},{2,3},{3,4},{4,5},{5,6},{6,7},{7,8},{8,9},{9,10},{10,1... | collective-permute-start | bytes 101384 | tf_op jit(solution)/shard_map/ppermute | solution.py:19
  355.7 14.2 %collective-permute-start.51 = (f32[66,1,128]{2,1,0:T(1,128)S(1)}, f32[66,1,128]{2,1,0:T(1,128)S(1)}, u32[]{:S(2)}, u32[]{:S(2)}) collective-permute-start(f32[66,1,128]{2,1,0:T(1,128)S(1)} %get-tuple-element.11), channel_id=1, source_target_pairs={{1,0},{2,1},{3,2},{4,3},{5,4},{6,5},{7,6},{8,7},{9,8},{10,9},{11,1... | collective-permute-start | bytes 101384 | tf_op jit(solution)/shard_map/ppermute | solution.py:22
  383.1 14.2 %collective-permute-start.55 = (f32[66,1,128]{2,1,0:T(1,128)S(1)}, f32[66,1,128]{2,1,0:T(1,128)S(1)}, u32[]{:S(2)}, u32[]{:S(2)}) collective-permute-start(f32[66,1,128]{2,1,0:T(1,128)S(1)} %get-tuple-element.9), channel_id=1, source_target_pairs={{1,0},{2,1},{3,2},{4,3},{5,4},{6,5},{7,6},{8,7},{9,8},{10,9},{11,1... | collective-permute-start | bytes 101384 | tf_op jit(solution)/shard_map/ppermute | solution.py:22
  (32 other events, 253.6 us)
where the time goes:
time: 406 us; the launch traced here: 402 us
  starting transfers between devices  174 us (43%)
  waiting for transfers between devices  161 us (40%)
  other arithmetic  60 us (15%)
  local copies, waits for them, and re-layouts  5.87 us (1%)
    ppermute x28, waiting for transfers between devices, with_halo(): lax.ppermute(lax.slice_in_dim(block, 0, width, axis=dim), axis, backward)  161 us
    ppermute x28, starting transfers between devices, with_halo(): lax.ppermute(lax.slice_in_dim(block, 0, width, axis=dim), axis, backward)  102 us
    ppermute x28, starting transfers between devices, with_halo(): lax.ppermute(lax.slice_in_dim(block, block.shape[dim] - width, None, axis...  71.2 us
    add x12, other arithmetic, sweep_once(): values + 0.8 * (load + neighbour_sum(padded) - (4.0 + mass_here) * values...  35.4 us
    sub x1, other arithmetic, per_device(): source_terms + neighbour_sum(with_halo(values, (('band', 0), ('lane', 1))...  9.31 us
  transfers between devices with their start and end apart: 56, of which 26 were waited for; matrix products, arithmetic and copies ran while one was open for 1% of the time, Pallas kernels for 0%

commit v1 on v0

v1 whole, which is shorter than its diff:
```python
import jax
import jax.numpy as jnp
from jax import lax
from jax.experimental import pallas as pl
from jax.experimental.pallas import tpu as pltpu
from jax.sharding import PartitionSpec as P

CASES = 128
BEFORE = 3
AFTER = 3
INNER = 13
N = 64
M = N // 2
DU = BEFORE + 1
DW = BEFORE
DV = AFTER
DC = INNER + 1
DM = INNER

PF, YF, XF = 88, 4, 8
SIZE_F = (N + 2 * YF) * PF
PC, YC, XC = 72, 14, 16
SIZE_C = (M + 2 * YC) * PC

SIDES = ((0, -1), (0, 1), (-1, 0), (1, 0), (-1, -1), (-1, 1), (1, -1), (1, 1))
MESH = pl.DeviceIdType.MESH


class Grid:
    def __init__(self, size, pitch, y_off, x_off):
        self.size, self.pitch, self.y_off, self.x_off = size, pitch, y_off, x_off

    def at(self, y, x):
        return (y + self.y_off) * self.pitch + x + self.x_off


FINE = Grid(N, PF, YF, XF)
COARSE = Grid(M, PC, YC, XC)


def pieces(grid, side, depth, sending):
    sy, sx = side
    n = grid.size

    def span(sign, count):
        if sending:
            return n - count if sign > 0 else 0
        return n if sign > 0 else -count

    if sy == 0:
        x0 = span(sx, depth)
        return [(grid.at(0, x0 + i), n, grid.pitch) for i in range(depth)]
    if sx == 0:
        y0 = span(sy, depth)
        return [(grid.at(y0 + i, 0), n, 1) for i in range(depth)]
    runs = []
    for dx in range(1, depth):
        if sending:
            x = n - dx if sx > 0 else dx - 1
        else:
            x = n - 1 + dx if sx > 0 else -dx
        count = depth - dx
        runs.append((grid.at(span(sy, count), x), count, grid.pitch))
    return runs


def message_rows(parts, side):
    total = sum(
        count for grid, depth in parts for _, count, _ in pieces(grid, side, depth, True)
    )
    return -(-total // 8) * 8


def rows(start, count, stride):
    return pl.ds(start, count) if stride == 1 else pl.ds(start, count, stride=stride)


def pack(buffer, refs, parts, side):
    at = 0
    for ref, (grid, depth) in zip(refs, parts):
        for start, count, stride in pieces(grid, side, depth, True):
            buffer[pl.ds(at, count), :] = ref[rows(start, count, stride), :]
            at += count


def unpack(buffer, refs, parts, side):
    at = 0
    for ref, (grid, depth) in zip(refs, parts):
        for start, count, stride in pieces(grid, side, depth, False):
            ref[rows(start, count, stride), :] = buffer[pl.ds(at, count), :]
            at += count


def clear(ref, grid, side, depth):
    sy, sx = side
    n = grid.size
    if sy == 0:
        for i in range(depth):
            x = n + i if sx > 0 else -1 - i
            count = n + 2 * grid.y_off
            ref[pl.ds(grid.at(-grid.y_off, x), count, stride=grid.pitch), :] = jnp.zeros(
                (count, CASES), jnp.float32
            )
    else:
        y0 = n if sy > 0 else -depth
        count = depth * grid.pitch
        ref[pl.ds(grid.at(y0, -grid.x_off), count), :] = jnp.zeros((count, CASES), jnp.float32)


PART_A = ((FINE, DU), (FINE, DW), (FINE, DW))
PART_M = ((COARSE, DM),)
PART_B = ((COARSE, DC),)
PART_V = ((FINE, DV),)
STAGES = (PART_A, PART_M, PART_B, PART_V)


def sweep(grid, src, dst, gain, base, groups, y_low, y_high, store_at=None, unroll=4):
    store_at = store_at or grid.at
    blocks = -(-(y_high - y_low) // unroll)

    def block(i, carry):
        y = jnp.minimum(y_low + i * unroll, y_high - unroll)
        row = grid.at(y, 0)
        out_row = store_at(y, 0)
        out_pitch = store_at(1, 0) - store_at(0, 0)
        for x0, width in groups:

            def load(ref, dy, x):
                return ref[pl.ds(row + dy * grid.pitch + x0 + x, 8, stride=width), :]

            left = [load(src, k, -1) for k in range(unroll)]
            here = [load(src, k, 0) for k in range(unroll)]
            for x in range(width):
                right = [load(src, k, x + 1) for k in range(unroll)]
                above = load(src, -1, x)
                below = load(src, unroll, x)
                for k in range(unroll):
                    up = here[k - 1] if k else above
                    down = here[k + 1] if k + 1 < unroll else below
                    around = (left[k] + right[k]) + (up + down)
                    new = (
                        0.2 * here[k] + load(base, k, x) + load(gain, k, x) * around
                    )
                    dst[pl.ds(out_row + k * out_pitch + x0 + x, 8, stride=width), :] = new
                left, here = here, right
        return carry

    lax.fori_loop(0, blocks, block, 0)


def kernel(source_hbm, values_hbm, mass_hbm, out_ref, source, start, mass, u0, u1, gain, base,
           coarse_gain, c0, c1, coarse_base, *rest):
    counts = len(STAGES) * len(SIDES)
    send_bufs, recv_bufs = rest[:counts], rest[counts : 2 * counts]
    load_sem, send_sem, recv_sem = rest[2 * counts :]
    band, lane = lax.axis_index("band"), lax.axis_index("lane")
    bands, lanes = lax.axis_size("band"), lax.axis_size("lane")

    loads = [
        pltpu.make_async_copy(src, dst, load_sem.at[i])
        for i, (src, dst) in enumerate(
            ((mass_hbm, mass), (source_hbm, source), (values_hbm, start))
        )
    ]
    for copy in loads:
        copy.start()

    exists, targets = [], []
    for sy, sx in SIDES:
        y, x = band + sy, lane + sx
        exists.append((y >= 0) & (y < bands) & (x >= 0) & (x < lanes))
        targets.append({"band": y, "lane": x})

    barrier = pltpu.get_barrier_semaphore()
    for there, target in zip(exists, targets):

        @pl.when(there)
        def _():
            pl.semaphore_signal(barrier, inc=1, device_id=target, device_id_type=MESH)

    for k in range(4):

        @pl.when(jnp.logical_not(exists[k]))
        def _():
            for ref, grid, depth in (
                (u0, FINE, DU), (gain, FINE, DW), (base, FINE, DW),
                (coarse_gain, COARSE, DM), (coarse_base, COARSE, DC),
            ):
                clear(ref, grid, SIDES[k], depth)

    loads[0].wait()

    def coarse_row(y, carry):
        for x in range(0, M, 8):
            total = None
            for dy in range(2):
                for dx in range(2):
                    part = mass[pl.ds((2 * y + dy) * N + 2 * x + dx, 8, stride=2), :]
                    total = part if total is None else total + part
            at = pl.multiple_of(COARSE.at(y, x), 8)
            coarse_gain[pl.ds(at, 8), :] = 0.8 / (4.0 + 0.5 * total)
        return carry

    lax.fori_loop(0, M, coarse_row, 0)
    loads[1].wait()
    loads[2].wait()

    def fine_row(y, carry):
        for x in range(0, N, 8):
            here = pl.ds(pl.multiple_of(y * N + x, 8), 8)
            there = pl.ds(pl.multiple_of(FINE.at(y, x), 8), 8)
            factor = 0.8 / (4.0 + mass[here, :])
            gain[there, :] = factor
            base[there, :] = factor * source[here, :]
            u0[there, :] = start[here, :]
        return carry

    lax.fori_loop(0, N, fine_row, 0)

    def copy_of(stage, k, arriving=False):
        at = stage * len(SIDES) + k
        sy, sx = SIDES[k]
        over = at if arriving else stage * len(SIDES) + SIDES.index((-sy, -sx))
        return pltpu.make_async_remote_copy(
            send_bufs[at], recv_bufs[over], send_sem.at[at], recv_sem.at[over],
            device_id=targets[k], device_id_type=MESH,
        )

    def send(stage, refs):
        for k, side in enumerate(SIDES):

            @pl.when(exists[k])
            def _():
                pack(send_bufs[stage * len(SIDES) + k], refs, STAGES[stage], side)
                copy_of(stage, k).start()

    def receive(stage, refs):
        for k, side in enumerate(SIDES):

            @pl.when(exists[k])
            def _():
                copy_of(stage, k, arriving=True).wait_recv()
                unpack(recv_bufs[stage * len(SIDES) + k], refs, STAGES[stage], side)

    total = jnp.int32(0)
    for there in exists:
        total = total + there.astype(jnp.int32)
    pl.semaphore_wait(barrier, total)

    send(0, (u0, gain, base))
    send(1, (coarse_gain,))
    receive(0, (u0, gain, base))

    wide = ((-DU, 9),)
    sweep(FINE, u0, u1, gain, base, wide, -3, N + 3)
    sweep(FINE, u1, u0, gain, base, wide, -2, N + 2)
    sweep(FINE, u0, u1, gain, base, wide, -1, N + 1)

    def restrict_row(y, carry):
        for x in range(0, M, 8):

            def u_at(dy, dx):
                return u1[pl.ds(FINE.at(2 * y + dy, 2 * x + dx), 8, stride=2), :]

            def own(ref, dy, dx):
                return ref[pl.ds((2 * y + dy) * N + 2 * x + dx, 8, stride=2), :]

            block = {}
            for dy in range(2):
                for dx in range(2):
                    block[dy, dx] = u_at(dy, dx)
            total = None
            for dy in range(2):
                for dx in range(2):
                    here = block[dy, dx]
                    around = (u_at(dy, -1 if dx == 0 else 2) + u_at(-1 if dy == 0 else 2, dx)) + (
                        block[dy, 1 - dx] + block[1 - dy, dx]
                    )
                    defect = (own(source, dy, dx) + around) - (4.0 + own(mass, dy, dx)) * here
                    total = defect if total is None else total + defect
            at = pl.multiple_of(COARSE.at(y, x), 8)
            coarse_base[pl.ds(at, 8), :] = coarse_gain[pl.ds(at, 8), :] * (0.5 * total)
        return carry

    lax.fori_loop(0, M, restrict_row, 0)
    send(2, (coarse_base,))
    send(3, (u1,))
    receive(1, (coarse_gain,))
    receive(2, (coarse_base,))

    src, dst = coarse_base, c0
    for step in range(1, INNER):
        depth = DC - step
        span = M + 2 * depth
        if span > 56:
            groups = ((-depth, 4), (-depth + 32, 4))
        else:
            groups = ((-depth, -(-span // 8)),)
        sweep(COARSE, src, dst, coarse_gain, coarse_base, groups, -depth, M + depth)
        src, dst = dst, (c1 if dst is c0 else c0)
    coarse = src

    for k in range(4):

        @pl.when(jnp.logical_not(exists[k]))
        def _():
            clear(u1, FINE, SIDES[k], DV)

    receive(3, (u1,))

    def prolong_row(i, carry):
        y = i - 2
        for x in (-2, 6, 14, 22, M - 6):
            add = coarse[pl.ds(COARSE.at(y, x), 8), :]
            for dy in range(2):
                for dx in range(2):
                    at = pl.ds(FINE.at(2 * y + dy, 2 * x + dx), 8, stride=2)
                    u0[at, :] = u1[at, :] + add
        return carry

    lax.fori_loop(0, M + 4, prolong_row, 0)
    sweep(FINE, u0, u1, gain, base, wide, -2, N + 2)
    sweep(FINE, u1, u0, gain, base, wide, -1, N + 1)
    sweep(FINE, u0, out_ref, gain, base, ((0, 4), (32, 4)), 0, N, store_at=lambda y, x: y * N + x)

    for stage in range(len(STAGES)):
        for k in range(len(SIDES)):

            @pl.when(exists[k])
            def _():
                copy_of(stage, k).wait_send()


def per_device(source_terms, initial_values, absorption):
    shape = source_terms.shape
    flat = [x.reshape(N * N, CASES) for x in (source_terms, initial_values, absorption)]
    vmem = lambda count: pltpu.VMEM((count, CASES), jnp.float32)
    buffers = [vmem(message_rows(parts, side)) for parts in STAGES for side in SIDES]
    result = pl.pallas_call(
        kernel,
        out_shape=jax.ShapeDtypeStruct((N * N, CASES), jnp.float32),
        in_specs=[pl.BlockSpec(memory_space=pl.ANY)] * 3,
        out_specs=pl.BlockSpec(memory_space=pltpu.VMEM),
        scratch_shapes=[vmem(N * N)] * 3
        + [vmem(SIZE_F)] * 4
        + [vmem(SIZE_C)] * 4
        + buffers
        + buffers
        + [
            pltpu.SemaphoreType.DMA((3,)),
            pltpu.SemaphoreType.DMA((len(buffers),)),
            pltpu.SemaphoreType.DMA((len(buffers),)),
        ],
        compiler_params=pltpu.CompilerParams(
            collective_id=0, has_side_effects=True, vmem_limit_bytes=56 << 20
        ),
        name="cycle",
    )(*flat)
    return result.reshape(shape)


def solution(mesh):
    placed = P(("shift", "band"), "lane", None)
    return jax.shard_map(
        per_device,
        mesh=mesh,
        in_specs=(placed,) * 3,
        out_specs=placed,
        check_vma=False,
    )
```

time: 406 us -> 83.8 us (0.21)
  starting transfers between devices: 174 us -> 0 us
  waiting for transfers between devices: 161 us -> 0 us
  Pallas kernels: 0 us -> 79.6 us
  other arithmetic: 60 us -> 0 us
    ppermute x56 -> x0, starting transfers between devices: 174 us -> none  [the longest x28 102 us: with_halo(): lax.ppermute(lax.slice_in_dim(block, 0, width, axis=dim), axis, backward)]
    ppermute x56 -> x0, waiting for transfers between devices: 161 us -> none  [the longest x28 161 us: with_halo(): lax.ppermute(lax.slice_in_dim(block, 0, width, axis=dim), axis, backward)]
    pallas_call x0 -> x1, Pallas kernels: none -> 79.6 us  [per_device(): pl.pallas_call(kernel, out_shape=jax.ShapeDtypeStruct((N * N, CASES), jnp...]
    add x13 -> x0, other arithmetic: 36 us -> none  [the longest x12 35.4 us: sweep_once(): values + 0.8 * (load + neighbour_sum(padded) - (4.0 + mass_here) * values...]
    sub x1 -> x0, other arithmetic: 9.31 us -> none  [per_device(): source_terms + neighbour_sum(with_halo(values, (('band', 0), ('lane', 1))...]
    select_n x6 -> x0, other arithmetic: 7.3 us -> none  [per_device(): once = jnp.where(without_rim(inside), once, 0.0)]
    reduce_sum x2 -> x0, other arithmetic: 4.89 us -> none  [block_means(): return jnp.mean(cut, axis=(1, 3))]
  transfers between devices with their start and end apart: 56 -> 0, of which waited for: 26 -> 0; matrix products, arithmetic and copies ran while one was open for 1% -> 0% of each run, Pallas kernels for 0% -> 0%
where the time goes in v1:
time: 83.8 us; the launch traced here: 82.7 us
  Pallas kernels  79.6 us (95%)
  local copies, waits for them, and re-layouts  3.16 us (4%)
    pallas_call x1, Pallas kernels, per_device(): pl.pallas_call(kernel, out_shape=jax.ShapeDtypeStruct((N * N, CASES), jnp...  79.6 us
    unnamed x1, local copies, waits for them, and re-layouts  3.16 us

profile of v1, /device:TPU:54, one launch (start us, length us, event | category | flops | bytes accessed | tf_op | source)
XLA Modules:
  0.0 82.7 jit_solution(16425753801175472456)
XLA Ops:
  0.0 79.6 %cycle.1 = f32[4096,128]{1,0:T(8,128)} custom-call(f32[4096,128]{1,0:T(8,128)} %bitcast.5, f32[4096,128]{1,0:T(8,128)} %bitcast.6, f32[4096,128]{1,0:T(8,128)} %bitcast.7), custom_call_target="tpu_custom_call" | custom-call | tf_op jit(solution)/shard_map/cycle/pallas_call | solution.py:339
  79.6 3.2 %copy.5 = f32[64,64,128]{2,1,0:T(8,128)} copy(f32[64,64,128]{2,1,0:T(8,128)} %bitcast.4) | data formatting | bytes 4194304

commit v2 on v1

--- a/solution.py
+++ b/solution.py
@@ -22,8 +22,19 @@
 PC, YC, XC = 72, 14, 16
 SIZE_C = (M + 2 * YC) * PC
 
+SLOW = ((7, 1, 3), (8, 0, 12))
+CHUNKS = (3, 3, 3, 1)
+
 SIDES = ((0, -1), (0, 1), (-1, 0), (1, 0), (-1, -1), (-1, 1), (1, -1), (1, 1))
 MESH = pl.DeviceIdType.MESH
+
+
+def split(stage):
+    whole = message_rows(STAGES[stage], (0, 1))
+    corners = 2 * message_rows(STAGES[stage], (1, 1))
+    each = (whole + corners) // 2 // CHUNKS[stage] // 8 * 8
+    first = whole - each * CHUNKS[stage]
+    return first, [(first + i * each, each) for i in range(CHUNKS[stage])]
 
 
 class Grid:
@@ -152,7 +163,8 @@
            coarse_gain, c0, c1, coarse_base, *rest):
     counts = len(STAGES) * len(SIDES)
     send_bufs, recv_bufs = rest[:counts], rest[counts : 2 * counts]
-    load_sem, send_sem, recv_sem = rest[2 * counts :]
+    held = rest[2 * counts : 2 * counts + len(STAGES)]
+    load_sem, send_sem, recv_sem, hop_sems = rest[2 * counts + len(STAGES) :]
     band, lane = lax.axis_index("band"), lax.axis_index("lane")
     bands, lanes = lax.axis_size("band"), lax.axis_size("lane")
 
@@ -177,6 +189,17 @@
         @pl.when(there)
         def _():
             pl.semaphore_signal(barrier, inc=1, device_id=target, device_id_type=MESH)
+
+    for far, side, between in SLOW:
+        other = far + (1 if side else -1)
+
+        @pl.when(lane == between)
+        def _():
+            pl.semaphore_signal(barrier, inc=1, device_id={"lane": jnp.int32(far)}, device_id_type=MESH)
+
+        @pl.when(lane == other)
+        def _():
+            pl.semaphore_signal(barrier, inc=1, device_id={"lane": jnp.int32(between)}, device_id_type=MESH)
 
     for k in range(4):
 
@@ -226,29 +249,102 @@
             device_id=targets[k], device_id_type=MESH,
         )
 
+    hops = [(stage, i) for stage in range(len(STAGES)) for i in range(CHUNKS[stage])]
+
+    def hop(stage, i, source_of, target, lane_to, leg):
+        at = hops.index((stage, i))
+        return pltpu.make_async_remote_copy(
+            source_of, target, hop_sems.at[leg, 0, at], hop_sems.at[leg, 1, at],
+            device_id={"lane": jnp.int32(lane_to)}, device_id_type=MESH,
+        )
+
+    def hops_of(leg, stage, far, side, between):
+        first, chunks = split(stage)
+        other = far + (1 if side else -1)
+        out = []
+        for i, (start, count) in enumerate(chunks):
+            here = held[stage].at[pl.ds(start - first, count)]
+            if leg == 0:
+                sent = send_bufs[stage * len(SIDES) + side].at[pl.ds(start, count)]
+                out.append(hop(stage, i, sent, here, between, 0))
+            else:
+                got = recv_bufs[stage * len(SIDES) + 1 - side].at[pl.ds(start, count)]
+                out.append(hop(stage, i, here, got, other, 1))
+        return out
+
+    def straight(stage, k, arriving=False):
+        at = stage * len(SIDES) + k
+        over = at if arriving else at + 1 - 2 * k
+        part = pl.ds(0, split(stage)[0])
+        return pltpu.make_async_remote_copy(
+            send_bufs[at].at[part], recv_bufs[over].at[part], send_sem.at[at], recv_sem.at[over],
+            device_id=targets[k], device_id_type=MESH,
+        )
+
+    slow = [lane == far for far, _, _ in SLOW]
+    slow_side = {side: i for i, (_, side, _) in enumerate(SLOW)}
+    whole = [
+        there & jnp.logical_not(slow[slow_side[k]]) if k in slow_side else there
+        for k, there in enumerate(exists)
+    ]
+
     def send(stage, refs):
-        for k, side in enumerate(SIDES):
+        for k in (1, 0, 4, 5, 6, 7, 2, 3):
 
             @pl.when(exists[k])
             def _():
-                pack(send_bufs[stage * len(SIDES) + k], refs, STAGES[stage], side)
+                pack(send_bufs[stage * len(SIDES) + k], refs, STAGES[stage], SIDES[k])
+
+            if k in slow_side:
+
+                @pl.when(slow[slow_side[k]])
+                def _():
+                    for first in hops_of(0, stage, *SLOW[slow_side[k]]):
+                        first.start()
+                    straight(stage, k).start()
+
+            @pl.when(whole[k])
+            def _():
                 copy_of(stage, k).start()
 
+    def pass_on(stage):
+        for entry in SLOW:
+
+            @pl.when(lane == entry[2])
+            def _():
+                for first, second in zip(hops_of(0, stage, *entry), hops_of(1, stage, *entry)):
+                    first.wait_recv()
+                    second.start()
+
     def receive(stage, refs):
-        for k, side in enumerate(SIDES):
+        for k in (2, 3, 4, 5, 6, 7, 0, 1):
+            if k in slow_side:
+
+                @pl.when(slow[slow_side[k]])
+                def _():
+                    straight(stage, k, arriving=True).wait_recv()
+                    for second in hops_of(1, stage, *SLOW[1 - slow_side[k]]):
+                        second.wait_recv()
+
+            @pl.when(whole[k])
+            def _():
+                copy_of(stage, k, arriving=True).wait_recv()
 
             @pl.when(exists[k])
             def _():
-                copy_of(stage, k, arriving=True).wait_recv()
-                unpack(recv_bufs[stage * len(SIDES) + k], refs, STAGES[stage], side)
+                unpack(recv_bufs[stage * len(SIDES) + k], refs, STAGES[stage], SIDES[k])
 
     total = jnp.int32(0)
     for there in exists:
         total = total + there.astype(jnp.int32)
+    for far, _, between in SLOW:
+        total = total + (lane == far).astype(jnp.int32) + (lane == between).astype(jnp.int32)
     pl.semaphore_wait(barrier, total)
 
     send(0, (u0, gain, base))
     send(1, (coarse_gain,))
+    pass_on(0)
+    pass_on(1)
     receive(0, (u0, gain, base))
 
     wide = ((-DU, 9),)
@@ -285,6 +381,8 @@
     lax.fori_loop(0, M, restrict_row, 0)
     send(2, (coarse_base,))
     send(3, (u1,))
+    pass_on(2)
+    pass_on(3)
     receive(1, (coarse_gain,))
     receive(2, (coarse_base,))
 
@@ -326,9 +424,24 @@
     for stage in range(len(STAGES)):
         for k in range(len(SIDES)):
 
-            @pl.when(exists[k])
+            if k in slow_side:
+
+                @pl.when(slow[slow_side[k]])
+                def _():
+                    for first in hops_of(0, stage, *SLOW[slow_side[k]]):
+                        first.wait_send()
+                    straight(stage, k).wait_send()
+
+            @pl.when(whole[k])
             def _():
                 copy_of(stage, k).wait_send()
+
+        for entry in SLOW:
+
+            @pl.when(lane == entry[2])
+            def _():
+                for second in hops_of(1, stage, *entry):
+                    second.wait_send()
 
 
 def per_device(source_terms, initial_values, absorption):
@@ -346,10 +459,12 @@
         + [vmem(SIZE_C)] * 4
         + buffers
         + buffers
+        + [vmem(sum(count for _, count in split(stage)[1])) for stage in range(len(STAGES))]
         + [
             pltpu.SemaphoreType.DMA((3,)),
             pltpu.SemaphoreType.DMA((len(buffers),)),
             pltpu.SemaphoreType.DMA((len(buffers),)),
+            pltpu.SemaphoreType.DMA((2, 2, sum(CHUNKS))),
         ],
         compiler_params=pltpu.CompilerParams(
             collective_id=0, has_side_effects=True, vmem_limit_bytes=56 << 20

time: 83.8 us -> 76.7 us (0.915); the launches traced: 82.7 us -> 76.5 us
  Pallas kernels: 79.6 us -> 73.3 us
    pallas_call x1, Pallas kernels: 79.6 us -> 73.3 us  [per_device(): pl.pallas_call(kernel, out_shape=jax.ShapeDtypeStruct((N * N, CASES), jnp...]
where the time goes in v2:
time: 76.7 us; the launch traced here: 76.5 us
  Pallas kernels  73.3 us (96%)
  local copies, waits for them, and re-layouts  3.16 us (4%)
    pallas_call x1, Pallas kernels, per_device(): pl.pallas_call(kernel, out_shape=jax.ShapeDtypeStruct((N * N, CASES), jnp...  73.3 us
    unnamed x1, local copies, waits for them, and re-layouts  3.16 us

profile of v2, /device:TPU:54, one launch (start us, length us, event | category | flops | bytes accessed | tf_op | source)
XLA Modules:
  0.0 76.5 jit_solution(3934011323251979482)
XLA Ops:
  0.0 73.3 %cycle.1 = f32[4096,128]{1,0:T(8,128)} custom-call(f32[4096,128]{1,0:T(8,128)} %bitcast.5, f32[4096,128]{1,0:T(8,128)} %bitcast.6, f32[4096,128]{1,0:T(8,128)} %bitcast.7), custom_call_target="tpu_custom_call" | custom-call | tf_op jit(solution)/shard_map/cycle/pallas_call | solution.py:452
  73.3 3.2 %copy.5 = f32[64,64,128]{2,1,0:T(8,128)} copy(f32[64,64,128]{2,1,0:T(8,128)} %bitcast.4) | data formatting | bytes 4194304

commit v3 on v2

--- a/solution.py
+++ b/solution.py
@@ -23,7 +23,7 @@
 SIZE_C = (M + 2 * YC) * PC
 
 SLOW = ((7, 1, 3), (8, 0, 12))
-CHUNKS = (3, 3, 3, 1)
+CHUNKS = (3, 2, 2, 0, 0)
 
 SIDES = ((0, -1), (0, 1), (-1, 0), (1, 0), (-1, -1), (-1, 1), (1, -1), (1, 1))
 MESH = pl.DeviceIdType.MESH
@@ -32,6 +32,8 @@
 def split(stage):
     whole = message_rows(STAGES[stage], (0, 1))
     corners = 2 * message_rows(STAGES[stage], (1, 1))
+    if not CHUNKS[stage]:
+        return whole, []
     each = (whole + corners) // 2 // CHUNKS[stage] // 8 * 8
     first = whole - each * CHUNKS[stage]
     return first, [(first + i * each, each) for i in range(CHUNKS[stage])]
@@ -49,35 +51,68 @@
 COARSE = Grid(M, PC, YC, XC)
 
 
-def pieces(grid, side, depth, sending):
-    sy, sx = side
+def runs(grid, side, boxes, sending):
+    def place(sign, low, high):
+        n = grid.size
+        if sign == 0:
+            return low, high - low
+        if sending:
+            return (n - high if sign > 0 else low - 1), high - low + 1
+        return (n - 1 + low if sign > 0 else -high), high - low + 1
+
+    out = []
+    for y_range, x_range, along_x in boxes:
+        y, height = place(side[0], *y_range)
+        x, width = place(side[1], *x_range)
+        if along_x:
+            out += [(grid.at(y + i, x), width, 1) for i in range(height)]
+        else:
+            out += [(grid.at(y, x + i), height, grid.pitch) for i in range(width)]
+    return out
+
+
+def whole_halo(grid, side, depth):
+    own = (0, grid.size)
+    if side[0] == 0:
+        return [(own, (1, depth), False)]
+    if side[1] == 0:
+        return [((1, depth), own, True)]
+    return [((1, depth - dx), (dx, dx), False) for dx in range(1, depth)]
+
+
+RIM = 2
+
+
+def early_halo(grid, side, depth):
+    own, deep = (RIM, grid.size - RIM), (RIM + 1, depth)
+    if side[0] == 0:
+        return [(own, deep, False)]
+    if side[1] == 0:
+        return [(deep, own, True)]
+    return [((RIM + 1, depth - dx), (dx, dx), False) for dx in range(RIM + 1, depth - RIM)]
+
+
+def late_halo(grid, side, depth):
     n = grid.size
-
-    def span(sign, count):
-        if sending:
-            return n - count if sign > 0 else 0
-        return n if sign > 0 else -count
-
-    if sy == 0:
-        x0 = span(sx, depth)
-        return [(grid.at(0, x0 + i), n, grid.pitch) for i in range(depth)]
-    if sx == 0:
-        y0 = span(sy, depth)
-        return [(grid.at(y0 + i, 0), n, 1) for i in range(depth)]
-    runs = []
-    for dx in range(1, depth):
-        if sending:
-            x = n - dx if sx > 0 else dx - 1
-        else:
-            x = n - 1 + dx if sx > 0 else -dx
-        count = depth - dx
-        runs.append((grid.at(span(sy, count), x), count, grid.pitch))
-    return runs
+    own, near, deep = (0, n), (1, RIM), (RIM + 1, depth)
+    ends = [(0, RIM), (n - RIM, n)]
+    if side[0] == 0:
+        return [(own, near, False)] + [(end, deep, True) for end in ends]
+    if side[1] == 0:
+        return [(near, own, True)] + [(deep, end, False) for end in ends]
+    return [((1, depth - dx), (dx, dx), False) for dx in range(1, RIM + 1)] + [
+        ((dy, dy), (RIM + 1, depth - dy), True) for dy in range(1, RIM + 1)
+    ]
+
+
+def pieces(part, side, sending):
+    grid, depth, boxes = part
+    return runs(grid, side, boxes(grid, side, depth), sending)
 
 
 def message_rows(parts, side):
     total = sum(
-        count for grid, depth in parts for _, count, _ in pieces(grid, side, depth, True)
+        count for part in parts for _, count, _ in pieces(part, side, True)
     )
     return -(-total // 8) * 8
 
@@ -88,16 +123,16 @@
 
 def pack(buffer, refs, parts, side):
     at = 0
-    for ref, (grid, depth) in zip(refs, parts):
-        for start, count, stride in pieces(grid, side, depth, True):
+    for ref, part in zip(refs, parts):
+        for start, count, stride in pieces(part, side, True):
             buffer[pl.ds(at, count), :] = ref[rows(start, count, stride), :]
             at += count
 
 
 def unpack(buffer, refs, parts, side):
     at = 0
-    for ref, (grid, depth) in zip(refs, parts):
-        for start, count, stride in pieces(grid, side, depth, False):
+    for ref, part in zip(refs, parts):
+        for start, count, stride in pieces(part, side, False):
             ref[rows(start, count, stride), :] = buffer[pl.ds(at, count), :]
             at += count
 
@@ -118,11 +153,13 @@
         ref[pl.ds(grid.at(y0, -grid.x_off), count), :] = jnp.zeros((count, CASES), jnp.float32)
 
 
-PART_A = ((FINE, DU), (FINE, DW), (FINE, DW))
-PART_M = ((COARSE, DM),)
-PART_B = ((COARSE, DC),)
-PART_V = ((FINE, DV),)
-STAGES = (PART_A, PART_M, PART_B, PART_V)
+STAGES = (
+    ((FINE, DU, whole_halo), (FINE, DW, whole_halo), (FINE, DW, whole_halo)),
+    ((COARSE, DM, whole_halo),),
+    ((COARSE, DC, early_halo),),
+    ((COARSE, DC, late_halo),),
+    ((FINE, DV, whole_halo),),
+)
 
 
 def sweep(grid, src, dst, gain, base, groups, y_low, y_high, store_at=None, unroll=4):
@@ -159,7 +196,26 @@
     lax.fori_loop(0, blocks, block, 0)
 
 
-def kernel(source_hbm, values_hbm, mass_hbm, out_ref, source, start, mass, u0, u1, gain, base,
+def sweep_strip(grid, src, dst, gain, base, x0, width):
+    def block(i, carry):
+        row = grid.at(8 * i, x0)
+
+        def load(ref, dy, x):
+            return ref[pl.ds(row + dy * grid.pitch + x, 8, stride=grid.pitch), :]
+
+        left, here = load(src, 0, -1), load(src, 0, 0)
+        for x in range(width):
+            right = load(src, 0, x + 1)
+            around = (left + right) + (load(src, -1, x) + load(src, 1, x))
+            new = 0.2 * here + load(base, 0, x) + load(gain, 0, x) * around
+            dst[pl.ds(row + x, 8, stride=grid.pitch), :] = new
+            left, here = here, right
+        return carry
+
+    lax.fori_loop(0, grid.size // 8, block, 0)
+
+
+def kernel(source_hbm, values_hbm, mass_hbm, out_ref, source, start, mass, u0, u1, u2, u3, gain, base,
            coarse_gain, c0, c1, coarse_base, *rest):
     counts = len(STAGES) * len(SIDES)
     send_bufs, recv_bufs = rest[:counts], rest[counts : 2 * counts]
@@ -224,9 +280,11 @@
             coarse_gain[pl.ds(at, 8), :] = 0.8 / (4.0 + 0.5 * total)
         return carry
 
-    lax.fori_loop(0, M, coarse_row, 0)
-    loads[1].wait()
-    loads[2].wait()
+    with jax.named_scope("coarse_setup"):
+        lax.fori_loop(0, M, coarse_row, 0)
+    with jax.named_scope("load"):
+        loads[1].wait()
+        loads[2].wait()
 
     def fine_row(y, carry):
         for x in range(0, N, 8):
@@ -238,7 +296,8 @@
             u0[there, :] = start[here, :]
         return carry
 
-    lax.fori_loop(0, N, fine_row, 0)
+    with jax.named_scope("fine_setup"):
+        lax.fori_loop(0, N, fine_row, 0)
 
     def copy_of(stage, k, arriving=False):
         at = stage * len(SIDES) + k
@@ -288,22 +347,23 @@
         for k, there in enumerate(exists)
     ]
 
-    def send(stage, refs):
+    def send(stage, refs, among=None):
+        among = lane >= 0 if among is None else among
         for k in (1, 0, 4, 5, 6, 7, 2, 3):
 
-            @pl.when(exists[k])
+            @pl.when(exists[k] & among)
             def _():
                 pack(send_bufs[stage * len(SIDES) + k], refs, STAGES[stage], SIDES[k])
 
             if k in slow_side:
 
-                @pl.when(slow[slow_side[k]])
+                @pl.when(slow[slow_side[k]] & among)
                 def _():
                     for first in hops_of(0, stage, *SLOW[slow_side[k]]):
                         first.start()
                     straight(stage, k).start()
 
-            @pl.when(whole[k])
+            @pl.when(whole[k] & among)
             def _():
                 copy_of(stage, k).start()
 
@@ -339,72 +399,102 @@
         total = total + there.astype(jnp.int32)
     for far, _, between in SLOW:
         total = total + (lane == far).astype(jnp.int32) + (lane == between).astype(jnp.int32)
-    pl.semaphore_wait(barrier, total)
-
-    send(0, (u0, gain, base))
-    send(1, (coarse_gain,))
-    pass_on(0)
-    pass_on(1)
-    receive(0, (u0, gain, base))
+    with jax.named_scope("barrier"):
+        pl.semaphore_wait(barrier, total)
+
+    with jax.named_scope("send_a"):
+        send(0, (u0, gain, base))
+    hurried = slow[0] | slow[1]
+    with jax.named_scope("send_m"):
+        send(1, (coarse_gain,), hurried)
 
     wide = ((-DU, 9),)
-    sweep(FINE, u0, u1, gain, base, wide, -3, N + 3)
-    sweep(FINE, u1, u0, gain, base, wide, -2, N + 2)
-    sweep(FINE, u0, u1, gain, base, wide, -1, N + 1)
-
-    def restrict_row(y, carry):
-        for x in range(0, M, 8):
-
-            def u_at(dy, dx):
-                return u1[pl.ds(FINE.at(2 * y + dy, 2 * x + dx), 8, stride=2), :]
-
-            def own(ref, dy, dx):
-                return ref[pl.ds((2 * y + dy) * N + 2 * x + dx, 8, stride=2), :]
-
-            block = {}
-            for dy in range(2):
-                for dx in range(2):
-                    block[dy, dx] = u_at(dy, dx)
-            total = None
-            for dy in range(2):
-                for dx in range(2):
-                    here = block[dy, dx]
-                    around = (u_at(dy, -1 if dx == 0 else 2) + u_at(-1 if dy == 0 else 2, dx)) + (
-                        block[dy, 1 - dx] + block[1 - dy, dx]
-                    )
-                    defect = (own(source, dy, dx) + around) - (4.0 + own(mass, dy, dx)) * here
-                    total = defect if total is None else total + defect
-            at = pl.multiple_of(COARSE.at(y, x), 8)
-            coarse_base[pl.ds(at, 8), :] = coarse_gain[pl.ds(at, 8), :] * (0.5 * total)
-        return carry
-
-    lax.fori_loop(0, M, restrict_row, 0)
-    send(2, (coarse_base,))
-    send(3, (u1,))
-    pass_on(2)
-    pass_on(3)
-    receive(1, (coarse_gain,))
-    receive(2, (coarse_base,))
-
-    src, dst = coarse_base, c0
-    for step in range(1, INNER):
-        depth = DC - step
-        span = M + 2 * depth
-        if span > 56:
-            groups = ((-depth, 4), (-depth + 32, 4))
-        else:
-            groups = ((-depth, -(-span // 8)),)
-        sweep(COARSE, src, dst, coarse_gain, coarse_base, groups, -depth, M + depth)
-        src, dst = dst, (c1 if dst is c0 else c0)
+
+    def restrict(low, high, groups):
+        def restrict_row(y, carry):
+            for x in groups:
+
+                def u_at(dy, dx):
+                    return u3[pl.ds(FINE.at(2 * y + dy, 2 * x + dx), 8, stride=2), :]
+
+                def own(ref, dy, dx):
+                    return ref[pl.ds((2 * y + dy) * N + 2 * x + dx, 8, stride=2), :]
+
+                block = {}
+                for dy in range(2):
+                    for dx in range(2):
+                        block[dy, dx] = u_at(dy, dx)
+                total = None
+                for dy in range(2):
+                    for dx in range(2):
+                        here = block[dy, dx]
+                        around = (
+                            u_at(dy, -1 if dx == 0 else 2) + u_at(-1 if dy == 0 else 2, dx)
+                        ) + (block[dy, 1 - dx] + block[1 - dy, dx])
+                        defect = (own(source, dy, dx) + around) - (4.0 + own(mass, dy, dx)) * here
+                        total = defect if total is None else total + defect
+                at = pl.multiple_of(COARSE.at(y, x), 8)
+                coarse_base[pl.ds(at, 8), :] = coarse_gain[pl.ds(at, 8), :] * (0.5 * total)
+            return carry
+
+        lax.fori_loop(low, high, restrict_row, 0)
+
+    with jax.named_scope("inside"):
+        sweep(FINE, u0, u1, gain, base, wide, 1, N - 1)
+        sweep(FINE, u1, u2, gain, base, wide, 2, N - 2)
+        sweep(FINE, u2, u3, gain, base, wide, 3, N - 3)
+        restrict(RIM, M - RIM, range(0, M, 8))
+    with jax.named_scope("send_e"):
+        send(2, (coarse_base,), hurried)
+    with jax.named_scope("pass_a"):
+        pass_on(0)
+    with jax.named_scope("receive_a"):
+        receive(0, (u0, gain, base))
+    with jax.named_scope("send_me"):
+        send(1, (coarse_gain,), jnp.logical_not(hurried))
+        send(2, (coarse_base,), jnp.logical_not(hurried))
+    with jax.named_scope("rim"):
+        for step, (src, dst) in enumerate(((u0, u1), (u1, u2), (u2, u3))):
+            for at in (step - 3, N - 1 - step):
+                sweep(FINE, src, dst, gain, base, wide, at, at + 4)
+                sweep_strip(FINE, src, dst, gain, base, at, 4)
+        restrict(0, RIM, range(0, M, 8))
+        restrict(M - RIM, M, range(0, M, 8))
+        restrict(RIM, M - RIM, (0, M - 8))
+    with jax.named_scope("send_l"):
+        send(3, (coarse_base,))
+        send(4, (u3,))
+    with jax.named_scope("pass_me"):
+        pass_on(1)
+        pass_on(2)
+    with jax.named_scope("receive_m"):
+        receive(1, (coarse_gain,))
+    with jax.named_scope("receive_e"):
+        receive(2, (coarse_base,))
+    with jax.named_scope("receive_l"):
+        receive(3, (coarse_base,))
+
+    with jax.named_scope("coarse"):
+        src, dst = coarse_base, c0
+        for step in range(1, INNER):
+            depth = DC - step
+            span = M + 2 * depth
+            if span > 56:
+                groups = ((-depth, 4), (-depth + 32, 4))
+            else:
+                groups = ((-depth, -(-span // 8)),)
+            sweep(COARSE, src, dst, coarse_gain, coarse_base, groups, -depth, M + depth)
+            src, dst = dst, (c1 if dst is c0 else c0)
     coarse = src
 
     for k in range(4):
 
         @pl.when(jnp.logical_not(exists[k]))
         def _():
-            clear(u1, FINE, SIDES[k], DV)
-
-    receive(3, (u1,))
+            clear(u3, FINE, SIDES[k], DV)
+
+    with jax.named_scope("receive_v"):
+        receive(4, (u3,))
 
     def prolong_row(i, carry):
         y = i - 2
@@ -413,13 +503,15 @@
             for dy in range(2):
                 for dx in range(2):
                     at = pl.ds(FINE.at(2 * y + dy, 2 * x + dx), 8, stride=2)
-                    u0[at, :] = u1[at, :] + add
+                    u0[at, :] = u3[at, :] + add
         return carry
 
-    lax.fori_loop(0, M + 4, prolong_row, 0)
-    sweep(FINE, u0, u1, gain, base, wide, -2, N + 2)
-    sweep(FINE, u1, u0, gain, base, wide, -1, N + 1)
-    sweep(FINE, u0, out_ref, gain, base, ((0, 4), (32, 4)), 0, N, store_at=lambda y, x: y * N + x)
+    with jax.named_scope("prolong"):
+        lax.fori_loop(0, M + 4, prolong_row, 0)
+    with jax.named_scope("after"):
+        sweep(FINE, u0, u1, gain, base, wide, -2, N + 2)
+        sweep(FINE, u1, u0, gain, base, wide, -1, N + 1)
+        sweep(FINE, u0, out_ref, gain, base, ((0, 4), (32, 4)), 0, N, store_at=lambda y, x: y * N + x)
 
     for stage in range(len(STAGES)):
         for k in range(len(SIDES)):
@@ -446,20 +538,23 @@
 
 def per_device(source_terms, initial_values, absorption):
     shape = source_terms.shape
-    flat = [x.reshape(N * N, CASES) for x in (source_terms, initial_values, absorption)]
+    flat = [
+        pltpu.with_memory_space_constraint(x.reshape(N * N, CASES), pltpu.HBM)
+        for x in (source_terms, initial_values, absorption)
+    ]
     vmem = lambda count: pltpu.VMEM((count, CASES), jnp.float32)
     buffers = [vmem(message_rows(parts, side)) for parts in STAGES for side in SIDES]
     result = pl.pallas_call(
         kernel,
-        out_shape=jax.ShapeDtypeStruct((N * N, CASES), jnp.float32),
-        in_specs=[pl.BlockSpec(memory_space=pl.ANY)] * 3,
+        out_shape=pltpu.VMEM((N * N, CASES), jnp.float32),
+        in_specs=[pl.BlockSpec(memory_space=pltpu.HBM)] * 3,
         out_specs=pl.BlockSpec(memory_space=pltpu.VMEM),
         scratch_shapes=[vmem(N * N)] * 3
-        + [vmem(SIZE_F)] * 4
+        + [vmem(SIZE_F)] * 6
         + [vmem(SIZE_C)] * 4
         + buffers
         + buffers
-        + [vmem(sum(count for _, count in split(stage)[1])) for stage in range(len(STAGES))]
+        + [vmem(8 + sum(count for _, count in split(stage)[1])) for stage in range(len(STAGES))]
         + [
             pltpu.SemaphoreType.DMA((3,)),
             pltpu.SemaphoreType.DMA((len(buffers),)),
@@ -467,7 +562,7 @@
             pltpu.SemaphoreType.DMA((2, 2, sum(CHUNKS))),
         ],
         compiler_params=pltpu.CompilerParams(
-            collective_id=0, has_side_effects=True, vmem_limit_bytes=56 << 20
+            collective_id=0, has_side_effects=True, vmem_limit_bytes=48 << 20
         ),
         name="cycle",
     )(*flat)

time: 76.7 us -> 68.2 us (0.89)
  Pallas kernels: 73.3 us -> 66.8 us
  local copies, waits for them, and re-layouts: 3.16 us -> 1.32 us
    pallas_call x1, Pallas kernels: 73.3 us -> 66.8 us  [per_device(): pl.pallas_call(kernel, out_shape=pltpu.VMEM((N * N, CASES), jnp.float32),...]
    unnamed x1, local copies, waits for them, and re-layouts: 3.16 us -> 1.32 us
where the time goes in v3:
time: 68.2 us; the launch traced here: 68.1 us
  Pallas kernels  66.8 us (98%)
  local copies, waits for them, and re-layouts  1.32 us (2%)
    pallas_call x1, Pallas kernels, per_device(): pl.pallas_call(kernel, out_shape=pltpu.VMEM((N * N, CASES), jnp.float32),...  66.8 us

profile of v3, /device:TPU:54, one launch (start us, length us, event | category | flops | bytes accessed | tf_op | source)
XLA Modules:
  0.0 68.1 jit_solution(8061487149940334912)
XLA Ops:
  0.0 66.8 %cycle.1 = f32[4096,128]{1,0:T(8,128)S(1)} custom-call(f32[4096,128]{1,0:T(8,128)} %bitcast.5, f32[4096,128]{1,0:T(8,128)} %bitcast.6, f32[4096,128]{1,0:T(8,128)} %bitcast.7), custom_call_target="tpu_custom_call" | custom-call | tf_op jit(solution)/shard_map/cycle/pallas_call | solution.py:547
  66.8 1.3 %copy.5 = f32[64,64,128]{2,1,0:T(8,128)} copy(f32[64,64,128]{2,1,0:T(8,128)S(1)} %bitcast.4) | data formatting | bytes 4194304

commit v4 on v3

--- a/solution.py
+++ b/solution.py
@@ -22,21 +22,37 @@
 PC, YC, XC = 72, 14, 16
 SIZE_C = (M + 2 * YC) * PC
 
-SLOW = ((7, 1, 3), (8, 0, 12))
-CHUNKS = (3, 2, 2, 0, 0)
-
+SLOW = ((7, 1, 8, (4, 6, 5)), (8, 0, 7, (11, 9, 10)))
+CHUNKS = (
+    ((96, 96), (88, 88), (72, 72)),
+    ((136,), (128,), (112,)),
+    ((104,), (104,), (88,)),
+    ((), (), ()),
+    ((), (), ()),
+    ((), (), ()),
+    ((), (), ()),
+)
 SIDES = ((0, -1), (0, 1), (-1, 0), (1, 0), (-1, -1), (-1, 1), (1, -1), (1, 1))
 MESH = pl.DeviceIdType.MESH
 
 
 def split(stage):
-    whole = message_rows(STAGES[stage], (0, 1))
-    corners = 2 * message_rows(STAGES[stage], (1, 1))
-    if not CHUNKS[stage]:
-        return whole, []
-    each = (whole + corners) // 2 // CHUNKS[stage] // 8 * 8
-    first = whole - each * CHUNKS[stage]
-    return first, [(first + i * each, each) for i in range(CHUNKS[stage])]
+    first = message_rows(STAGES[stage], (0, 1)) - sum(sum(route) for route in CHUNKS[stage])
+    at, routes = first, []
+    for route in CHUNKS[stage]:
+        routes.append([])
+        for count in route:
+            routes[-1].append((at, count))
+            at += count
+    return first, routes
+
+
+HOPS = [
+    (stage, route, chunk)
+    for stage in range(len(CHUNKS))
+    for route in range(len(CHUNKS[stage]))
+    for chunk in range(len(CHUNKS[stage][route]))
+]
 
 
 class Grid:
@@ -52,18 +68,18 @@
 
 
 def runs(grid, side, boxes, sending):
-    def place(sign, low, high):
+    def place(sign, low, high, own):
         n = grid.size
         if sign == 0:
             return low, high - low
-        if sending:
+        if own:
             return (n - high if sign > 0 else low - 1), high - low + 1
         return (n - 1 + low if sign > 0 else -high), high - low + 1
 
     out = []
     for y_range, x_range, along_x in boxes:
-        y, height = place(side[0], *y_range)
-        x, width = place(side[1], *x_range)
+        y, height = place(side[0], *y_range, sending[0])
+        x, width = place(side[1], *x_range, sending[1])
         if along_x:
             out += [(grid.at(y + i, x), width, 1) for i in range(height)]
         else:
@@ -105,9 +121,25 @@
     ]
 
 
+def far_halo(grid, side, depth):
+    own = (0, grid.size)
+    if side[0] == 0:
+        return [(own, (2, depth), False)]
+    if side[1] == 0:
+        return [((2, depth), own, True)]
+    return whole_halo(grid, side, depth)
+
+
 def pieces(part, side, sending):
-    grid, depth, boxes = part
-    return runs(grid, side, boxes(grid, side, depth), sending)
+    grid, depth, boxes, corners = part
+    if not corners:
+        return runs(grid, side, boxes(grid, side, depth), (sending, sending))
+    both = [(sy, side[1]) for sy in (-1, 1)]
+    return [
+        run
+        for corner in both
+        for run in runs(grid, corner, boxes(grid, corner, depth), (False, sending))
+    ]
 
 
 def message_rows(parts, side):
@@ -154,12 +186,17 @@
 
 
 STAGES = (
-    ((FINE, DU, whole_halo), (FINE, DW, whole_halo), (FINE, DW, whole_halo)),
-    ((COARSE, DM, whole_halo),),
-    ((COARSE, DC, early_halo),),
-    ((COARSE, DC, late_halo),),
-    ((FINE, DV, whole_halo),),
+    tuple((FINE, depth, whole_halo, False) for depth in (DU, DW, DW)),
+    ((COARSE, DM, whole_halo, False),),
+    ((COARSE, DC, early_halo, False),),
+    ((COARSE, DC, late_halo, False),),
+    ((FINE, DV, far_halo, False),),
+    ((COARSE, DM, whole_halo, True),),
+    ((COARSE, DC, early_halo, True),),
 )
+ALL = (1, 0, 2, 3, 4, 5, 6, 7)
+STAGE_SIDES = (ALL, ALL, ALL, ALL, ALL, ALL[:2], ALL[:2])
+CORNERS_BY_SIDES = (1, 2)
 
 
 def sweep(grid, src, dst, gain, base, groups, y_low, y_high, store_at=None, unroll=4):
@@ -246,16 +283,17 @@
         def _():
             pl.semaphore_signal(barrier, inc=1, device_id=target, device_id_type=MESH)
 
-    for far, side, between in SLOW:
-        other = far + (1 if side else -1)
-
-        @pl.when(lane == between)
-        def _():
-            pl.semaphore_signal(barrier, inc=1, device_id={"lane": jnp.int32(far)}, device_id_type=MESH)
-
-        @pl.when(lane == other)
-        def _():
-            pl.semaphore_signal(barrier, inc=1, device_id={"lane": jnp.int32(between)}, device_id_type=MESH)
+    def tell(lane_to):
+        pl.semaphore_signal(
+            barrier, inc=1, device_id={"lane": jnp.int32(lane_to)}, device_id_type=MESH
+        )
+
+    for far, _, _, betweens in SLOW:
+        for between in betweens:
+
+            @pl.when(lane == between)
+            def _():
+                tell(far)
 
     for k in range(4):
 
@@ -308,28 +346,30 @@
             device_id=targets[k], device_id_type=MESH,
         )
 
-    hops = [(stage, i) for stage in range(len(STAGES)) for i in range(CHUNKS[stage])]
-
-    def hop(stage, i, source_of, target, lane_to, leg):
-        at = hops.index((stage, i))
-        return pltpu.make_async_remote_copy(
-            source_of, target, hop_sems.at[leg, 0, at], hop_sems.at[leg, 1, at],
-            device_id={"lane": jnp.int32(lane_to)}, device_id_type=MESH,
-        )
-
-    def hops_of(leg, stage, far, side, between):
-        first, chunks = split(stage)
-        other = far + (1 if side else -1)
+    def hops_of(leg, stage, entry, route):
+        _, side, other, betweens = entry
+        chunks = split(stage)[1][route]
         out = []
         for i, (start, count) in enumerate(chunks):
-            here = held[stage].at[pl.ds(start - first, count)]
+            at = HOPS.index((stage, route, i))
+            here = held[stage].at[pl.ds(start - chunks[0][0], count)]
             if leg == 0:
-                sent = send_bufs[stage * len(SIDES) + side].at[pl.ds(start, count)]
-                out.append(hop(stage, i, sent, here, between, 0))
+                source = send_bufs[stage * len(SIDES) + side].at[pl.ds(start, count)]
+                target, lane_to = here, betweens[route]
             else:
-                got = recv_bufs[stage * len(SIDES) + 1 - side].at[pl.ds(start, count)]
-                out.append(hop(stage, i, here, got, other, 1))
+                source, lane_to = here, other
+                target = recv_bufs[stage * len(SIDES) + 1 - side].at[pl.ds(start, count)]
+            out.append(
+                pltpu.make_async_remote_copy(
+                    source, target, hop_sems.at[leg, 0, at], hop_sems.at[leg, 1, at],
+                    device_id={"lane": jnp.int32(lane_to)}, device_id_type=MESH,
+                )
+            )
         return out
+
+    def all_hops(leg, stage, entry):
+        per_route = [hops_of(leg, stage, entry, route) for route in range(len(entry[3]))]
+        return [copy for copies in per_route for copy in copies]
 
     def straight(stage, k, arriving=False):
         at = stage * len(SIDES) + k
@@ -340,73 +380,112 @@
             device_id=targets[k], device_id_type=MESH,
         )
 
-    slow = [lane == far for far, _, _ in SLOW]
-    slow_side = {side: i for i, (_, side, _) in enumerate(SLOW)}
+    slow = [lane == entry[0] for entry in SLOW]
+    slow_side = {entry[1]: i for i, entry in enumerate(SLOW)}
     whole = [
         there & jnp.logical_not(slow[slow_side[k]]) if k in slow_side else there
         for k, there in enumerate(exists)
     ]
 
-    def send(stage, refs, among=None):
-        among = lane >= 0 if among is None else among
-        for k in (1, 0, 4, 5, 6, 7, 2, 3):
-
-            @pl.when(exists[k] & among)
+    def crosses(k):
+        for i, entry in enumerate(SLOW):
+            if SIDES[k][1] == entry[2] - entry[0]:
+                return slow[i]
+        return None
+
+    def in_one(stage, k):
+        if k in slow_side:
+            return whole[k]
+        if stage in CORNERS_BY_SIDES and k >= 4:
+            return exists[k] & crosses(k)
+        return exists[k]
+
+    def in_parts(stage, k):
+        if k not in slow_side or any(corners for _, _, _, corners in STAGES[stage]):
+            return None
+        return slow[slow_side[k]]
+
+    def send_across(stage, refs):
+        for k in STAGE_SIDES[stage]:
+            if crosses(k) is None:
+                continue
+
+            @pl.when(exists[k] & crosses(k))
             def _():
                 pack(send_bufs[stage * len(SIDES) + k], refs, STAGES[stage], SIDES[k])
-
-            if k in slow_side:
-
-                @pl.when(slow[slow_side[k]] & among)
-                def _():
-                    for first in hops_of(0, stage, *SLOW[slow_side[k]]):
-                        first.start()
+                if k in slow_side:
+                    for copy in all_hops(0, stage, SLOW[slow_side[k]]):
+                        copy.start()
                     straight(stage, k).start()
-
-            @pl.when(whole[k] & among)
+                else:
+                    copy_of(stage, k).start()
+
+    relays = jnp.bool_(False)
+    for entry in SLOW:
+        for between in entry[3]:
+            relays = relays | (lane == between)
+
+    def send(stage, refs, sides=None, among=None):
+        for k in STAGE_SIDES[stage] if sides is None else sides:
+            there = exists[k] if among is None else exists[k] & among
+            if crosses(k) is not None:
+                there = there & jnp.logical_not(crosses(k))
+
+            @pl.when(there)
             def _():
+                pack(send_bufs[stage * len(SIDES) + k], refs, STAGES[stage], SIDES[k])
                 copy_of(stage, k).start()
 
     def pass_on(stage):
         for entry in SLOW:
-
-            @pl.when(lane == entry[2])
+            for route, between in enumerate(entry[3]):
+                if CHUNKS[stage][route]:
+
+                    @pl.when(lane == between)
+                    def _():
+                        for first, second in zip(
+                            hops_of(0, stage, entry, route), hops_of(1, stage, entry, route)
+                        ):
+                            first.wait_recv()
+                            second.start()
+
+    def receive(stage, refs, sides=(2, 3, 4, 5, 6, 7, 0, 1)):
+        for k in sides:
+            if k not in STAGE_SIDES[stage]:
+                continue
+
+            @pl.when(in_one(stage, k))
             def _():
-                for first, second in zip(hops_of(0, stage, *entry), hops_of(1, stage, *entry)):
-                    first.wait_recv()
-                    second.start()
-
-    def receive(stage, refs):
-        for k in (2, 3, 4, 5, 6, 7, 0, 1):
-            if k in slow_side:
-
-                @pl.when(slow[slow_side[k]])
+                copy_of(stage, k, arriving=True).wait_recv()
+                if in_parts(stage, k) is None:
+                    unpack(recv_bufs[stage * len(SIDES) + k], refs, STAGES[stage], SIDES[k])
+
+            if in_parts(stage, k) is not None:
+
+                @pl.when(in_parts(stage, k))
                 def _():
                     straight(stage, k, arriving=True).wait_recv()
-                    for second in hops_of(1, stage, *SLOW[1 - slow_side[k]]):
-                        second.wait_recv()
-
-            @pl.when(whole[k])
-            def _():
-                copy_of(stage, k, arriving=True).wait_recv()
-
-            @pl.when(exists[k])
-            def _():
-                unpack(recv_bufs[stage * len(SIDES) + k], refs, STAGES[stage], SIDES[k])
+                    for copy in all_hops(1, stage, SLOW[1 - slow_side[k]]):
+                        copy.wait_recv()
+
+                @pl.when(exists[k])
+                def _():
+                    unpack(recv_bufs[stage * len(SIDES) + k], refs, STAGES[stage], SIDES[k])
 
     total = jnp.int32(0)
     for there in exists:
         total = total + there.astype(jnp.int32)
-    for far, _, between in SLOW:
-        total = total + (lane == far).astype(jnp.int32) + (lane == between).astype(jnp.int32)
+    for far, _, _, betweens in SLOW:
+        total = total + (lane == far).astype(jnp.int32) * len(betweens)
     with jax.named_scope("barrier"):
         pl.semaphore_wait(barrier, total)
 
+    with jax.named_scope("cross_am"):
+        send_across(0, (u0, gain, base))
+        send_across(1, (coarse_gain,))
     with jax.named_scope("send_a"):
-        send(0, (u0, gain, base))
-    hurried = slow[0] | slow[1]
-    with jax.named_scope("send_m"):
-        send(1, (coarse_gain,), hurried)
+        send(0, (u0, gain, base), (1, 0, 4, 5, 6, 7))
+        send(0, (u0, gain, base), (2, 3), jnp.logical_not(relays))
 
     wide = ((-DU, 9),)
 
@@ -444,15 +523,21 @@
         sweep(FINE, u1, u2, gain, base, wide, 2, N - 2)
         sweep(FINE, u2, u3, gain, base, wide, 3, N - 3)
         restrict(RIM, M - RIM, range(0, M, 8))
-    with jax.named_scope("send_e"):
-        send(2, (coarse_base,), hurried)
+    with jax.named_scope("cross_e"):
+        send_across(2, (coarse_base,))
     with jax.named_scope("pass_a"):
         pass_on(0)
+    with jax.named_scope("send_a_late"):
+        send(0, (u0, gain, base), (2, 3), relays)
+    with jax.named_scope("pass_m"):
+        pass_on(1)
+    with jax.named_scope("pass_e"):
+        pass_on(2)
     with jax.named_scope("receive_a"):
         receive(0, (u0, gain, base))
     with jax.named_scope("send_me"):
-        send(1, (coarse_gain,), jnp.logical_not(hurried))
-        send(2, (coarse_base,), jnp.logical_not(hurried))
+        send(1, (coarse_gain,), ALL[:4])
+        send(2, (coarse_base,), ALL[:4])
     with jax.named_scope("rim"):
         for step, (src, dst) in enumerate(((u0, u1), (u1, u2), (u2, u3))):
             for at in (step - 3, N - 1 - step):
@@ -462,15 +547,22 @@
         restrict(M - RIM, M, range(0, M, 8))
         restrict(RIM, M - RIM, (0, M - 8))
     with jax.named_scope("send_l"):
+        send_across(3, (coarse_base,))
         send(3, (coarse_base,))
+        send_across(4, (u3,))
         send(4, (u3,))
-    with jax.named_scope("pass_me"):
-        pass_on(1)
-        pass_on(2)
+    with jax.named_scope("receive_my"):
+        receive(1, (coarse_gain,), (2, 3))
+        send(5, (coarse_gain,))
+    with jax.named_scope("receive_ey"):
+        receive(2, (coarse_base,), (2, 3))
+        send(6, (coarse_base,))
     with jax.named_scope("receive_m"):
-        receive(1, (coarse_gain,))
+        receive(1, (coarse_gain,), (4, 5, 6, 7, 0, 1))
+        receive(5, (coarse_gain,))
     with jax.named_scope("receive_e"):
-        receive(2, (coarse_base,))
+        receive(2, (coarse_base,), (4, 5, 6, 7, 0, 1))
+        receive(6, (coarse_base,))
     with jax.named_scope("receive_l"):
         receive(3, (coarse_base,))
 
@@ -514,26 +606,28 @@
         sweep(FINE, u0, out_ref, gain, base, ((0, 4), (32, 4)), 0, N, store_at=lambda y, x: y * N + x)
 
     for stage in range(len(STAGES)):
-        for k in range(len(SIDES)):
-
-            if k in slow_side:
-
-                @pl.when(slow[slow_side[k]])
+        for k in STAGE_SIDES[stage]:
+
+            if in_parts(stage, k) is not None:
+
+                @pl.when(in_parts(stage, k))
                 def _():
-                    for first in hops_of(0, stage, *SLOW[slow_side[k]]):
-                        first.wait_send()
+                    for copy in all_hops(0, stage, SLOW[slow_side[k]]):
+                        copy.wait_send()
                     straight(stage, k).wait_send()
 
-            @pl.when(whole[k])
+            @pl.when(in_one(stage, k))
             def _():
                 copy_of(stage, k).wait_send()
 
         for entry in SLOW:
-
-            @pl.when(lane == entry[2])
-            def _():
-                for second in hops_of(1, stage, *entry):
-                    second.wait_send()
+            for route, between in enumerate(entry[3]):
+                if CHUNKS[stage][route]:
+
+                    @pl.when(lane == between)
+                    def _():
+                        for copy in hops_of(1, stage, entry, route):
+                            copy.wait_send()
 
 
 def per_device(source_terms, initial_values, absorption):
@@ -543,7 +637,11 @@
         for x in (source_terms, initial_values, absorption)
     ]
     vmem = lambda count: pltpu.VMEM((count, CASES), jnp.float32)
-    buffers = [vmem(message_rows(parts, side)) for parts in STAGES for side in SIDES]
+    buffers = [
+        vmem(message_rows(parts, side) if k in sides else 8)
+        for parts, sides in zip(STAGES, STAGE_SIDES)
+        for k, side in enumerate(SIDES)
+    ]
     result = pl.pallas_call(
         kernel,
         out_shape=pltpu.VMEM((N * N, CASES), jnp.float32),
@@ -554,12 +652,12 @@
         + [vmem(SIZE_C)] * 4
         + buffers
         + buffers
-        + [vmem(8 + sum(count for _, count in split(stage)[1])) for stage in range(len(STAGES))]
+        + [vmem(max(8, *(sum(route) for route in routes))) for routes in CHUNKS]
         + [
             pltpu.SemaphoreType.DMA((3,)),
             pltpu.SemaphoreType.DMA((len(buffers),)),
             pltpu.SemaphoreType.DMA((len(buffers),)),
-            pltpu.SemaphoreType.DMA((2, 2, sum(CHUNKS))),
+            pltpu.SemaphoreType.DMA((2, 2, len(HOPS))),
         ],
         compiler_params=pltpu.CompilerParams(
             collective_id=0, has_side_effects=True, vmem_limit_bytes=48 << 20

time: 68.2 us -> 56.2 us (0.82)
  Pallas kernels: 66.8 us -> 54.8 us
    pallas_call x1, Pallas kernels: 66.8 us -> 54.8 us  [per_device(): pl.pallas_call(kernel, out_shape=pltpu.VMEM((N * N, CASES), jnp.float32),...]
where the time goes in v4:
time: 56.2 us; the launch traced here: 56.1 us
  Pallas kernels  54.8 us (98%)
  local copies, waits for them, and re-layouts  1.32 us (2%)
    pallas_call x1, Pallas kernels, per_device(): pl.pallas_call(kernel, out_shape=pltpu.VMEM((N * N, CASES), jnp.float32),...  54.8 us
    unnamed x1, local copies, waits for them, and re-layouts  1.32 us

profile of v4, /device:TPU:54, one launch (start us, length us, event | category | flops | bytes accessed | tf_op | source)
XLA Modules:
  0.0 56.1 jit_solution(3853328273141846214)
XLA Ops:
  0.0 54.8 %cycle.1 = f32[4096,128]{1,0:T(8,128)S(1)} custom-call(f32[4096,128]{1,0:T(8,128)} %bitcast.5, f32[4096,128]{1,0:T(8,128)} %bitcast.6, f32[4096,128]{1,0:T(8,128)} %bitcast.7), custom_call_target="tpu_custom_call" | custom-call | tf_op jit(solution)/shard_map/cycle/pallas_call | solution.py:645
  54.8 1.3 %copy.5 = f32[64,64,128]{2,1,0:T(8,128)} copy(f32[64,64,128]{2,1,0:T(8,128)S(1)} %bitcast.4) | data formatting | bytes 4194304

commit v5 on v4

--- a/solution.py
+++ b/solution.py
@@ -36,6 +36,16 @@
 MESH = pl.DeviceIdType.MESH
 
 
+def sem_of(stage, k):
+    return SEMS.index(sem_key(stage, k))
+
+
+def sem_key(stage, k):
+    if stage in CORNERS_BY_SIDES and k >= 4:
+        return stage, "corner", SIDES[k][0]
+    return stage, "side", k
+
+
 def split(stage):
     first = message_rows(STAGES[stage], (0, 1)) - sum(sum(route) for route in CHUNKS[stage])
     at, routes = first, []
@@ -96,6 +106,7 @@
     return [((1, depth - dx), (dx, dx), False) for dx in range(1, depth)]
 
 
+PARTS = 4
 RIM = 2
 
 
@@ -195,8 +206,10 @@
     ((COARSE, DC, early_halo, True),),
 )
 ALL = (1, 0, 2, 3, 4, 5, 6, 7)
-STAGE_SIDES = (ALL, ALL, ALL, ALL, ALL, ALL[:2], ALL[:2])
+CORNERS_FIRST = (1, 0, 4, 5, 6, 7, 2, 3)
+STAGE_SIDES = (CORNERS_FIRST, ALL, ALL, CORNERS_FIRST, CORNERS_FIRST, ALL[:2], ALL[:2])
 CORNERS_BY_SIDES = (1, 2)
+SEMS = list(dict.fromkeys(sem_key(stage, k) for stage, ks in enumerate(STAGE_SIDES) for k in ks))
 
 
 def sweep(grid, src, dst, gain, base, groups, y_low, y_high, store_at=None, unroll=4):
@@ -257,7 +270,7 @@
     counts = len(STAGES) * len(SIDES)
     send_bufs, recv_bufs = rest[:counts], rest[counts : 2 * counts]
     held = rest[2 * counts : 2 * counts + len(STAGES)]
-    load_sem, send_sem, recv_sem, hop_sems = rest[2 * counts + len(STAGES) :]
+    load_sem, send_sem, recv_sem, hop_sems, store_sem, result = rest[2 * counts + len(STAGES) :]
     band, lane = lax.axis_index("band"), lax.axis_index("lane")
     bands, lanes = lax.axis_size("band"), lax.axis_size("lane")
 
@@ -342,7 +355,8 @@
         sy, sx = SIDES[k]
         over = at if arriving else stage * len(SIDES) + SIDES.index((-sy, -sx))
         return pltpu.make_async_remote_copy(
-            send_bufs[at], recv_bufs[over], send_sem.at[at], recv_sem.at[over],
+            send_bufs[at], recv_bufs[over],
+            send_sem.at[sem_of(stage, k)], recv_sem.at[sem_of(stage, over % len(SIDES))],
             device_id=targets[k], device_id_type=MESH,
         )
 
@@ -361,7 +375,7 @@
                 target = recv_bufs[stage * len(SIDES) + 1 - side].at[pl.ds(start, count)]
             out.append(
                 pltpu.make_async_remote_copy(
-                    source, target, hop_sems.at[leg, 0, at], hop_sems.at[leg, 1, at],
+                    source, target, hop_sems.at[leg, at], hop_sems.at[leg, at],
                     device_id={"lane": jnp.int32(lane_to)}, device_id_type=MESH,
                 )
             )
@@ -376,7 +390,8 @@
         over = at if arriving else at + 1 - 2 * k
         part = pl.ds(0, split(stage)[0])
         return pltpu.make_async_remote_copy(
-            send_bufs[at].at[part], recv_bufs[over].at[part], send_sem.at[at], recv_sem.at[over],
+            send_bufs[at].at[part], recv_bufs[over].at[part],
+            send_sem.at[sem_of(stage, k)], recv_sem.at[sem_of(stage, over % len(SIDES))],
             device_id=targets[k], device_id_type=MESH,
         )
 
@@ -386,6 +401,8 @@
         there & jnp.logical_not(slow[slow_side[k]]) if k in slow_side else there
         for k, there in enumerate(exists)
     ]
+
+    hurried = slow[0] | slow[1]
 
     def crosses(k):
         for i, entry in enumerate(SLOW):
@@ -484,8 +501,7 @@
         send_across(0, (u0, gain, base))
         send_across(1, (coarse_gain,))
     with jax.named_scope("send_a"):
-        send(0, (u0, gain, base), (1, 0, 4, 5, 6, 7))
-        send(0, (u0, gain, base), (2, 3), jnp.logical_not(relays))
+        send(0, (u0, gain, base))
 
     wide = ((-DU, 9),)
 
@@ -525,19 +541,20 @@
         restrict(RIM, M - RIM, range(0, M, 8))
     with jax.named_scope("cross_e"):
         send_across(2, (coarse_base,))
+        send(1, (coarse_gain,), ALL[:4], hurried)
     with jax.named_scope("pass_a"):
         pass_on(0)
-    with jax.named_scope("send_a_late"):
-        send(0, (u0, gain, base), (2, 3), relays)
     with jax.named_scope("pass_m"):
         pass_on(1)
+    with jax.named_scope("send_m_early"):
+        send(1, (coarse_gain,), ALL[:4], relays)
+    with jax.named_scope("receive_a"):
+        receive(0, (u0, gain, base))
     with jax.named_scope("pass_e"):
         pass_on(2)
-    with jax.named_scope("receive_a"):
-        receive(0, (u0, gain, base))
     with jax.named_scope("send_me"):
-        send(1, (coarse_gain,), ALL[:4])
-        send(2, (coarse_base,), ALL[:4])
+        send(1, (coarse_gain,), ALL[:4], jnp.logical_not(relays | hurried))
+        send(2, (coarse_base,), ALL[:4], jnp.logical_not(hurried))
     with jax.named_scope("rim"):
         for step, (src, dst) in enumerate(((u0, u1), (u1, u2), (u2, u3))):
             for at in (step - 3, N - 1 - step):
@@ -548,6 +565,7 @@
         restrict(RIM, M - RIM, (0, M - 8))
     with jax.named_scope("send_l"):
         send_across(3, (coarse_base,))
+        send(2, (coarse_base,), ALL[:4], hurried)
         send(3, (coarse_base,))
         send_across(4, (u3,))
         send(4, (u3,))
@@ -603,8 +621,19 @@
     with jax.named_scope("after"):
         sweep(FINE, u0, u1, gain, base, wide, -2, N + 2)
         sweep(FINE, u1, u0, gain, base, wide, -1, N + 1)
-        sweep(FINE, u0, out_ref, gain, base, ((0, 4), (32, 4)), 0, N, store_at=lambda y, x: y * N + x)
-
+        stores = []
+        for i in range(PARTS):
+            low, high = i * N // PARTS, (i + 1) * N // PARTS
+            sweep(
+                FINE, u0, result, gain, base, ((0, 4), (32, 4)), low, high,
+                store_at=lambda y, x: y * N + x,
+            )
+            part = pl.ds(low * N, (high - low) * N)
+            stores.append(pltpu.make_async_copy(result.at[part], out_ref.at[part], store_sem.at[i]))
+            stores[-1].start()
+
+    for store in stores:
+        store.wait()
     for stage in range(len(STAGES)):
         for k in STAGE_SIDES[stage]:
 
@@ -646,7 +675,7 @@
         kernel,
         out_shape=pltpu.VMEM((N * N, CASES), jnp.float32),
         in_specs=[pl.BlockSpec(memory_space=pltpu.HBM)] * 3,
-        out_specs=pl.BlockSpec(memory_space=pltpu.VMEM),
+        out_specs=pl.BlockSpec(memory_space=pl.ANY),
         scratch_shapes=[vmem(N * N)] * 3
         + [vmem(SIZE_F)] * 6
         + [vmem(SIZE_C)] * 4
@@ -655,9 +684,11 @@
         + [vmem(max(8, *(sum(route) for route in routes))) for routes in CHUNKS]
         + [
             pltpu.SemaphoreType.DMA((3,)),
-            pltpu.SemaphoreType.DMA((len(buffers),)),
-            pltpu.SemaphoreType.DMA((len(buffers),)),
-            pltpu.SemaphoreType.DMA((2, 2, len(HOPS))),
+            pltpu.SemaphoreType.DMA((len(SEMS),)),
+            pltpu.SemaphoreType.DMA((len(SEMS),)),
+            pltpu.SemaphoreType.DMA((2, len(HOPS))),
+            pltpu.SemaphoreType.DMA((PARTS,)),
+            vmem(N * N),
         ],
         compiler_params=pltpu.CompilerParams(
             collective_id=0, has_side_effects=True, vmem_limit_bytes=48 << 20

time: 56.2 us -> 53.9 us (0.959)
  the two profiles are of different devices: /device:TPU:54 before, /device:TPU:20 now
where the time goes in v5:
time: 53.9 us; the launch traced here: 53.8 us
  Pallas kernels  52.5 us (97%)
  local copies, waits for them, and re-layouts  1.32 us (2%)
    pallas_call x1, Pallas kernels, per_device(): pl.pallas_call(kernel, out_shape=pltpu.VMEM((N * N, CASES), jnp.float32),...  52.5 us
    unnamed x1, local copies, waits for them, and re-layouts  1.32 us

profile of v5, /device:TPU:20, one launch (start us, length us, event | category | flops | bytes accessed | tf_op | source)
XLA Modules:
  0.0 53.8 jit_solution(7468448989431592908)
XLA Ops:
  0.0 52.5 %cycle.1 = f32[4096,128]{1,0:T(8,128)S(1)} custom-call(f32[4096,128]{1,0:T(8,128)} %bitcast.5, f32[4096,128]{1,0:T(8,128)} %bitcast.6, f32[4096,128]{1,0:T(8,128)} %bitcast.7), custom_call_target="tpu_custom_call" | custom-call | tf_op jit(solution)/shard_map/cycle/pallas_call | solution.py:674
  52.5 1.3 %copy.5 = f32[64,64,128]{2,1,0:T(8,128)} copy(f32[64,64,128]{2,1,0:T(8,128)S(1)} %bitcast.4) | data formatting | bytes 4194304

commit v6 on v5

--- a/solution.py
+++ b/solution.py
@@ -24,9 +24,9 @@
 
 SLOW = ((7, 1, 8, (4, 6, 5)), (8, 0, 7, (11, 9, 10)))
 CHUNKS = (
-    ((96, 96), (88, 88), (72, 72)),
-    ((136,), (128,), (112,)),
-    ((104,), (104,), (88,)),
+    ((104, 104,), (72, 72,), (88, 88,)),
+    ((144,), (136,), (136,)),
+    ((112,), (112,), (112,)),
     ((), (), ()),
     ((), (), ()),
     ((), (), ()),
@@ -212,9 +212,11 @@
 SEMS = list(dict.fromkeys(sem_key(stage, k) for stage, ks in enumerate(STAGE_SIDES) for k in ks))
 
 
-def sweep(grid, src, dst, gain, base, groups, y_low, y_high, store_at=None, unroll=4):
+def sweep(grid, src, dst, gain, base, groups, y_low, y_high, store_at=None):
     store_at = store_at or grid.at
-    blocks = -(-(y_high - y_low) // unroll)
+    count = y_high - y_low
+    unroll = min(range(min(count, 7), min(count, 10) + 1), key=lambda n: (-(-count // n) * n, -n))
+    blocks = -(-count // unroll)
 
     def block(i, carry):
         y = jnp.minimum(y_low + i * unroll, y_high - unroll)
@@ -433,7 +435,8 @@
                 if k in slow_side:
                     for copy in all_hops(0, stage, SLOW[slow_side[k]]):
                         copy.start()
-                    straight(stage, k).start()
+                    if split(stage)[0]:
+                        straight(stage, k).start()
                 else:
                     copy_of(stage, k).start()
 
@@ -481,7 +484,8 @@
 
                 @pl.when(in_parts(stage, k))
                 def _():
-                    straight(stage, k, arriving=True).wait_recv()
+                    if split(stage)[0]:
+                        straight(stage, k, arriving=True).wait_recv()
                     for copy in all_hops(1, stage, SLOW[1 - slow_side[k]]):
                         copy.wait_recv()
 
@@ -643,7 +647,8 @@
                 def _():
                     for copy in all_hops(0, stage, SLOW[slow_side[k]]):
                         copy.wait_send()
-                    straight(stage, k).wait_send()
+                    if split(stage)[0]:
+                        straight(stage, k).wait_send()
 
             @pl.when(in_one(stage, k))
             def _():

time: 53.9 us -> 51.4 us (0.954)
  the two profiles are of different devices: /device:TPU:20 before, /device:TPU:14 now
where the time goes in v6:
time: 51.4 us; the launch traced here: 51.3 us
  Pallas kernels  50 us (97%)
  local copies, waits for them, and re-layouts  1.32 us (3%)
    pallas_call x1, Pallas kernels, per_device(): pl.pallas_call(kernel, out_shape=pltpu.VMEM((N * N, CASES), jnp.float32),...  50 us
    unnamed x1, local copies, waits for them, and re-layouts  1.32 us

profile of v6, /device:TPU:14, one launch (start us, length us, event | category | flops | bytes accessed | tf_op | source)
XLA Modules:
  0.0 51.3 jit_solution(14934302725753378369)
XLA Ops:
  0.0 50.0 %cycle.1 = f32[4096,128]{1,0:T(8,128)S(1)} custom-call(f32[4096,128]{1,0:T(8,128)} %bitcast.5, f32[4096,128]{1,0:T(8,128)} %bitcast.6, f32[4096,128]{1,0:T(8,128)} %bitcast.7), custom_call_target="tpu_custom_call" | custom-call | tf_op jit(solution)/shard_map/cycle/pallas_call | solution.py:679
  50.0 1.3 %copy.5 = f32[64,64,128]{2,1,0:T(8,128)} copy(f32[64,64,128]{2,1,0:T(8,128)S(1)} %bitcast.4) | data formatting | bytes 4194304

commit v7 on v6

--- a/solution.py
+++ b/solution.py
@@ -24,9 +24,9 @@
 
 SLOW = ((7, 1, 8, (4, 6, 5)), (8, 0, 7, (11, 9, 10)))
 CHUNKS = (
-    ((104, 104,), (72, 72,), (88, 88,)),
-    ((144,), (136,), (136,)),
-    ((112,), (112,), (112,)),
+    ((104, 104,), (72, 72,), (80, 80,)),
+    ((152,), (128,), (136,)),
+    ((120,), (96,), (120,)),
     ((), (), ()),
     ((), (), ()),
     ((), (), ()),
@@ -248,23 +248,25 @@
     lax.fori_loop(0, blocks, block, 0)
 
 
-def sweep_strip(grid, src, dst, gain, base, x0, width):
-    def block(i, carry):
-        row = grid.at(8 * i, x0)
-
-        def load(ref, dy, x):
-            return ref[pl.ds(row + dy * grid.pitch + x, 8, stride=grid.pitch), :]
-
-        left, here = load(src, 0, -1), load(src, 0, 0)
-        for x in range(width):
-            right = load(src, 0, x + 1)
-            around = (left + right) + (load(src, -1, x) + load(src, 1, x))
-            new = 0.2 * here + load(base, 0, x) + load(gain, 0, x) * around
-            dst[pl.ds(row + x, 8, stride=grid.pitch), :] = new
-            left, here = here, right
+def sweep_strips(grid, src, dst, gain, base, starts, width, blocks=2):
+    def step(i, carry):
+        for j in range(blocks):
+            for x0 in starts:
+                row = grid.at(8 * (i * blocks + j), x0)
+
+                def load(ref, dy, x):
+                    return ref[pl.ds(row + dy * grid.pitch + x, 8, stride=grid.pitch), :]
+
+                left, here = load(src, 0, -1), load(src, 0, 0)
+                for x in range(width):
+                    right = load(src, 0, x + 1)
+                    around = (left + right) + (load(src, -1, x) + load(src, 1, x))
+                    new = 0.2 * here + load(base, 0, x) + load(gain, 0, x) * around
+                    dst[pl.ds(row + x, 8, stride=grid.pitch), :] = new
+                    left, here = here, right
         return carry
 
-    lax.fori_loop(0, grid.size // 8, block, 0)
+    lax.fori_loop(0, grid.size // 8 // blocks, step, 0)
 
 
 def kernel(source_hbm, values_hbm, mass_hbm, out_ref, source, start, mass, u0, u1, u2, u3, gain, base,
@@ -339,18 +341,25 @@
         loads[1].wait()
         loads[2].wait()
 
-    def fine_row(y, carry):
-        for x in range(0, N, 8):
-            here = pl.ds(pl.multiple_of(y * N + x, 8), 8)
-            there = pl.ds(pl.multiple_of(FINE.at(y, x), 8), 8)
-            factor = 0.8 / (4.0 + mass[here, :])
-            gain[there, :] = factor
-            base[there, :] = factor * source[here, :]
-            u0[there, :] = start[here, :]
-        return carry
+    def fine_cells(steps, cells):
+        def fine_step(i, carry):
+            for y, x in cells(i):
+                here = pl.ds(pl.multiple_of(y * N + x, 8), 8)
+                there = pl.ds(pl.multiple_of(FINE.at(y, x), 8), 8)
+                factor = 0.8 / (4.0 + mass[here, :])
+                gain[there, :] = factor
+                base[there, :] = factor * source[here, :]
+                u0[there, :] = start[here, :]
+            return carry
+
+        lax.fori_loop(0, steps, fine_step, 0)
 
     with jax.named_scope("fine_setup"):
-        lax.fori_loop(0, N, fine_row, 0)
+        fine_cells(DU, lambda i: [(y, x) for y in (i, N - DU + i) for x in range(0, N, 8)])
+        fine_cells(
+            (N - 2 * DU) // 8,
+            lambda i: [(DU + 8 * i + j, x) for j in range(8) for x in (0, N - 8)],
+        )
 
     def copy_of(stage, k, arriving=False):
         at = stage * len(SIDES) + k
@@ -509,9 +518,9 @@
 
     wide = ((-DU, 9),)
 
-    def restrict(low, high, groups):
-        def restrict_row(y, carry):
-            for x in groups:
+    def restrict(low, high, groups, each=1):
+        def restrict_rows(i, carry):
+            for y, x in [(low + i * each + j, x) for j in range(each) for x in groups]:
 
                 def u_at(dy, dx):
                     return u3[pl.ds(FINE.at(2 * y + dy, 2 * x + dx), 8, stride=2), :]
@@ -536,9 +545,13 @@
                 coarse_base[pl.ds(at, 8), :] = coarse_gain[pl.ds(at, 8), :] * (0.5 * total)
             return carry
 
-        lax.fori_loop(low, high, restrict_row, 0)
+        lax.fori_loop(0, (high - low) // each, restrict_rows, 0)
 
     with jax.named_scope("inside"):
+        fine_cells(
+            (N - 2 * DU) // 2,
+            lambda i: [(DU + 2 * i + j, x) for j in range(2) for x in range(8, N - 8, 8)],
+        )
         sweep(FINE, u0, u1, gain, base, wide, 1, N - 1)
         sweep(FINE, u1, u2, gain, base, wide, 2, N - 2)
         sweep(FINE, u2, u3, gain, base, wide, 3, N - 3)
@@ -546,30 +559,32 @@
     with jax.named_scope("cross_e"):
         send_across(2, (coarse_base,))
         send(1, (coarse_gain,), ALL[:4], hurried)
+        send(2, (coarse_base,), ALL[:4], hurried)
     with jax.named_scope("pass_a"):
         pass_on(0)
     with jax.named_scope("pass_m"):
         pass_on(1)
     with jax.named_scope("send_m_early"):
         send(1, (coarse_gain,), ALL[:4], relays)
+        send(2, (coarse_base,), ALL[:4], relays)
     with jax.named_scope("receive_a"):
         receive(0, (u0, gain, base))
     with jax.named_scope("pass_e"):
         pass_on(2)
     with jax.named_scope("send_me"):
         send(1, (coarse_gain,), ALL[:4], jnp.logical_not(relays | hurried))
-        send(2, (coarse_base,), ALL[:4], jnp.logical_not(hurried))
+        send(2, (coarse_base,), ALL[:4], jnp.logical_not(relays | hurried))
     with jax.named_scope("rim"):
         for step, (src, dst) in enumerate(((u0, u1), (u1, u2), (u2, u3))):
-            for at in (step - 3, N - 1 - step):
+            ends = (step - 3, N - 1 - step)
+            for at in ends:
                 sweep(FINE, src, dst, gain, base, wide, at, at + 4)
-                sweep_strip(FINE, src, dst, gain, base, at, 4)
+            sweep_strips(FINE, src, dst, gain, base, ends, 4)
         restrict(0, RIM, range(0, M, 8))
         restrict(M - RIM, M, range(0, M, 8))
-        restrict(RIM, M - RIM, (0, M - 8))
+        restrict(RIM, M - RIM, (0, M - 8), 2)
     with jax.named_scope("send_l"):
         send_across(3, (coarse_base,))
-        send(2, (coarse_base,), ALL[:4], hurried)
         send(3, (coarse_base,))
         send_across(4, (u3,))
         send(4, (u3,))

time: 51.4 us -> 50.8 us (0.988)
  the two profiles are of different devices: /device:TPU:14 before, /device:TPU:54 now
where the time goes in v7:
time: 50.8 us; the launch traced here: 49.8 us
  Pallas kernels  48.5 us (95%)
  local copies, waits for them, and re-layouts  1.32 us (3%)
    pallas_call x1, Pallas kernels, per_device(): pl.pallas_call(kernel, out_shape=pltpu.VMEM((N * N, CASES), jnp.float32),...  48.5 us
    unnamed x1, local copies, waits for them, and re-layouts  1.32 us

profile of v7, /device:TPU:54, one launch (start us, length us, event | category | flops | bytes accessed | tf_op | source)
XLA Modules:
  0.0 49.8 jit_solution(5050001147759879948)
XLA Ops:
  0.0 48.5 %cycle.1 = f32[4096,128]{1,0:T(8,128)S(1)} custom-call(f32[4096,128]{1,0:T(8,128)} %bitcast.5, f32[4096,128]{1,0:T(8,128)} %bitcast.6, f32[4096,128]{1,0:T(8,128)} %bitcast.7), custom_call_target="tpu_custom_call" | custom-call | tf_op jit(solution)/shard_map/cycle/pallas_call | solution.py:694
  48.5 1.3 %copy.5 = f32[64,64,128]{2,1,0:T(8,128)} copy(f32[64,64,128]{2,1,0:T(8,128)S(1)} %bitcast.4) | data formatting | bytes 4194304

commit v8 on v7

--- a/solution.py
+++ b/solution.py
@@ -18,9 +18,9 @@
 DM = INNER
 
 PF, YF, XF = 88, 4, 8
-SIZE_F = (N + 2 * YF) * PF
+SIZE_F = (N + 2 * YF + 8) * PF
 PC, YC, XC = 72, 14, 16
-SIZE_C = (M + 2 * YC) * PC
+SIZE_C = (M + 2 * YC + 8) * PC
 
 SLOW = ((7, 1, 8, (4, 6, 5)), (8, 0, 7, (11, 9, 10)))
 CHUNKS = (
@@ -279,7 +279,7 @@
     bands, lanes = lax.axis_size("band"), lax.axis_size("lane")
 
     loads = [
-        pltpu.make_async_copy(src, dst, load_sem.at[i])
+        pltpu.make_async_copy(src, dst.at[pl.ds(0, N * N)], load_sem.at[i])
         for i, (src, dst) in enumerate(
             ((mass_hbm, mass), (source_hbm, source), (values_hbm, start))
         )
@@ -365,8 +365,9 @@
         at = stage * len(SIDES) + k
         sy, sx = SIDES[k]
         over = at if arriving else stage * len(SIDES) + SIDES.index((-sy, -sx))
+        part = pl.ds(0, message_rows(STAGES[stage], SIDES[k]))
         return pltpu.make_async_remote_copy(
-            send_bufs[at], recv_bufs[over],
+            send_bufs[at].at[part], recv_bufs[over].at[part],
             send_sem.at[sem_of(stage, k)], recv_sem.at[sem_of(stage, over % len(SIDES))],
             device_id=targets[k], device_id_type=MESH,
         )
@@ -687,7 +688,7 @@
     ]
     vmem = lambda count: pltpu.VMEM((count, CASES), jnp.float32)
     buffers = [
-        vmem(message_rows(parts, side) if k in sides else 8)
+        vmem(message_rows(parts, side) + 8 if k in sides else 8)
         for parts, sides in zip(STAGES, STAGE_SIDES)
         for k, side in enumerate(SIDES)
     ]
@@ -696,7 +697,7 @@
         out_shape=pltpu.VMEM((N * N, CASES), jnp.float32),
         in_specs=[pl.BlockSpec(memory_space=pltpu.HBM)] * 3,
         out_specs=pl.BlockSpec(memory_space=pl.ANY),
-        scratch_shapes=[vmem(N * N)] * 3
+        scratch_shapes=[vmem(N * N + 8)] * 3
         + [vmem(SIZE_F)] * 6
         + [vmem(SIZE_C)] * 4
         + buffers
@@ -708,7 +709,7 @@
             pltpu.SemaphoreType.DMA((len(SEMS),)),
             pltpu.SemaphoreType.DMA((2, len(HOPS))),
             pltpu.SemaphoreType.DMA((PARTS,)),
-            vmem(N * N),
+            vmem(N * N + 8),
         ],
         compiler_params=pltpu.CompilerParams(
             collective_id=0, has_side_effects=True, vmem_limit_bytes=48 << 20

time: 50.8 us -> 50.8 us (level)
  no operation moved by 1% of the time
where the time goes in v8:
time: 50.8 us; the launch traced here: 49.8 us
  Pallas kernels  48.5 us (95%)
  local copies, waits for them, and re-layouts  1.32 us (3%)
    pallas_call x1, Pallas kernels, per_device(): pl.pallas_call(kernel, out_shape=pltpu.VMEM((N * N, CASES), jnp.float32),...  48.5 us
    unnamed x1, local copies, waits for them, and re-layouts  1.32 us

profile of v8, /device:TPU:54, one launch (start us, length us, event | category | flops | bytes accessed | tf_op | source)
XLA Modules:
  0.0 49.8 jit_solution(5718621584387465794)
XLA Ops:
  0.0 48.5 %cycle.1 = f32[4096,128]{1,0:T(8,128)S(1)} custom-call(f32[4096,128]{1,0:T(8,128)} %bitcast.5, f32[4096,128]{1,0:T(8,128)} %bitcast.6, f32[4096,128]{1,0:T(8,128)} %bitcast.7), custom_call_target="tpu_custom_call" | custom-call | tf_op jit(solution)/shard_map/cycle/pallas_call | solution.py:695
  48.5 1.3 %copy.5 = f32[64,64,128]{2,1,0:T(8,128)} copy(f32[64,64,128]{2,1,0:T(8,128)S(1)} %bitcast.4) | data formatting | bytes 4194304
